TPU v7x, 8 devices: a whole 2x2x1 slice. The times are simulated.
8 devices in a mesh: dp: 1 (over z), ep_b: 2 (over y), ep_a: 4 (over x, core).
Axes of the slice: x: 2, y: 2, z: 1, core: 2. Of those that a mesh axis runs over, the one named last changes fastest.
Arguments:
- tokens: bfloat16 [8, 8192, 1280], P(('dp', 'ep_b', 'ep_a'))
- expert_ids: int32 [8, 8192], P(('dp', 'ep_b', 'ep_a'))
- route_order: int32 [8, 8192], P(('dp', 'ep_b', 'ep_a'))
- w_route: bfloat16 [1280, 256], replicated
- expert_keys: bfloat16 [8, 256], replicated
- temperature: float32 [], replicated
- w_in: bfloat16 [8, 1280, 5120], P(('ep_b', 'ep_a'))
- b_in: bfloat16 [8, 5120], P(('ep_b', 'ep_a'))
- w_out: bfloat16 [8, 5120, 1280], P(('ep_b', 'ep_a'))
- b_out: bfloat16 [8, 1280], P(('ep_b', 'ep_a'))
Outputs:
- output: bfloat16 [8, 8192, 1280], P(('dp', 'ep_b', 'ep_a'))
All inputs are finite; a program needn't handle non-finite values.
Results may differ from a plain program's by a relative error of at most 0.0023964.
Values are sent between devices in bfloat16 or wider.
A program may use at most 1 GiB of HBM per device.

v0:
```python
import jax
import jax.numpy as jnp
from jax import lax
from jax.sharding import PartitionSpec as P

EXPERT_AXES = ("ep_b", "ep_a")


def route_local(tok_rows, id_row, order_row, w_route, expert_keys, value_a11, capacity):
    num_experts = expert_keys.shape[0]
    tok_dev = tok_rows.shape[0]
    keys_f32 = expert_keys.astype(jnp.float32)
    key_unit = keys_f32 / jnp.sqrt(jnp.sum(keys_f32 * keys_f32, axis=1, keepdims=True))
    projected = jnp.dot(tok_rows, w_route, preferred_element_type=jnp.float32)
    proj_unit = projected / jnp.sqrt(jnp.sum(projected * projected, axis=1, keepdims=True))
    router_prob = jax.nn.softmax(jnp.dot(proj_unit, key_unit.T) / value_a11, axis=1)
    expert_range = jnp.arange(num_experts, dtype=jnp.int32)[None, :]
    gate_prob = jnp.sum(jnp.where(id_row[:, None] == expert_range, router_prob, 0.0), axis=1)
    ranked_ids = jnp.take(id_row, order_row)
    ranked_hot = (ranked_ids[:, None] == expert_range).astype(jnp.int32)
    ranked_pos = jnp.sum(jnp.cumsum(ranked_hot, axis=0) * ranked_hot, axis=1) - 1
    ranked_slot = jnp.where(ranked_pos < capacity, ranked_ids * capacity + ranked_pos, num_experts * capacity)
    slot_source = jnp.full((num_experts * capacity,), tok_dev, jnp.int32).at[ranked_slot].set(order_row, mode="drop")
    dest_slot = jnp.zeros((tok_dev,), jnp.int32).at[order_row].set(ranked_slot)
    send_rows = jnp.take(tok_rows, slot_source, axis=0, mode="fill", fill_value=0)
    return send_rows, gate_prob, dest_slot


def expert_local(slot_rows, w_first, b_first, w_second, b_second):
    hidden = jnp.dot(slot_rows, w_first, preferred_element_type=jnp.float32) + b_first.astype(jnp.float32)
    hidden = jax.nn.gelu(hidden, approximate=False).astype(jnp.bfloat16)
    result = jnp.dot(hidden, w_second, preferred_element_type=jnp.float32) + b_second.astype(jnp.float32)
    return result.astype(jnp.bfloat16)


def combine_local(back_rows, dest_slot, gate_prob):
    picked = jnp.take(back_rows, dest_slot, axis=0, mode="fill", fill_value=0)
    return (gate_prob[:, None] * picked.astype(jnp.float32)).astype(jnp.bfloat16)


def solution(mesh):
    num_experts = mesh.shape["ep_b"] * mesh.shape["ep_a"]
    tok_spec = P(("dp",) + EXPERT_AXES)
    expert_spec = P(EXPERT_AXES)

    def device_step(tokens, expert_ids, route_order, w_route, expert_keys, value_a11, w_in, b_in, w_out, b_out):
        tok_dev, model_width = tokens.shape[1], tokens.shape[2]
        capacity = (5 * tok_dev + 4 * num_experts - 1) // (4 * num_experts)
        send_rows, gate_prob, dest_slot = route_local(tokens[0], expert_ids[0], route_order[0], w_route, expert_keys, value_a11, capacity)
        arrived = lax.all_to_all(send_rows.reshape(num_experts, capacity, model_width), EXPERT_AXES, 0, 0, tiled=True)
        expert_rows = expert_local(arrived.reshape(num_experts * capacity, model_width), w_in[0], b_in[0], w_out[0], b_out[0])
        returned = lax.all_to_all(expert_rows.reshape(num_experts, capacity, model_width), EXPERT_AXES, 0, 0, tiled=True)
        return combine_local(returned.reshape(num_experts * capacity, model_width), dest_slot, gate_prob)[None]

    return jax.shard_map(
        device_step,
        mesh=mesh,
        in_specs=(tok_spec, tok_spec, tok_spec, P(), P(), P(), expert_spec, expert_spec, expert_spec, expert_spec),
        out_specs=tok_spec,
        check_vma=False,
    )
```

profile of v0, /device:TPU:0, one launch (start us, length us, event | category | flops | bytes accessed | tf_op | source)
XLA Modules:
  0.0 1562.0 jit_solution(17601517675816714513)
XLA Ops:
  0.0 0.0 copy-start
  0.0 0.9 compare_select_fusion.1
  0.9 0.0 copy-start.2
  0.9 0.6 copy-done.2
  1.5 37.4 %gather_fusion = s32[8192]{0:T(1024)S(1)} fusion(s32[8192]{0:T(1024)} %bitcast.60, s32[8192]{0:T(1024)S(1)} %broadcast_clamp_fusion), kind=kCustom, calls=%fused_computation | custom fusion | bytes 98304 | tf_op jit(solution)/shard_map/jit(_take)/gather | solution.py:19
  38.8 0.8 bitcast_select_fusion.1
  39.6 2.4 reduce-window.6
  42.0 0.3 slice_reduce_fusion
  42.4 0.2 reduce-window.9
  42.6 0.1 add_bitcast_fusion
  42.7 0.8 and_select_fusion.1
  43.5 0.2 fusion.17
  43.7 0.6 add_select_fusion
  44.4 0.9 compare_select_fusion
  45.2 30.7 %scatter_custom_fusion.1 = s32[10240]{0:T(1024)S(1)} fusion(s32[8192]{0:T(1024)S(1)} %bitcast.72, s32[8192]{0:T(1024)} %bitcast.67, s32[]{:T(128)} %constant.43.clone.1), kind=kCustom, calls=%fused_computation.61 | custom fusion | bytes 41472 | tf_op jit(solution)/shard_map/scatter | solution.py:23
  76.0 0.1 broadcast_in_dim.69
  76.0 65.1 %gather_fusion.1 = bf16[10240,1280]{1,0:T(8,128)(2,1)} fusion(bf16[8192,1280]{1,0:T(8,128)(2,1)} %bitcast.62, s32[10240]{0:T(1024)S(1)} %fusion.20), kind=kCustom, calls=%fused_computation.1 | custom fusion | bytes 52469760 | tf_op jit(solution)/shard_map/jit(_take)/gather | solution.py:25
  141.2 0.0 copy-start.3
  141.2 0.0 copy-start.5
  141.2 18.5 %broadcast_select_fusion = bf16[8,1280,1280]{2,1,0:T(8,128)(2,1)} fusion(bf16[8,1280,1280]{2,1,0:T(8,128)(2,1)} %bitcast.63, pred[8,1280]{1,0:T(8,128)(4,1)S(1)} %broadcast_in_dim.69), kind=kLoop, calls=%fused_computation.26 | loop fusion | flops 13107200 | bytes 52439040 | tf_op jit(solution)/shard_map/jit(_take)/select_n | solution.py:25
  159.7 5.2 all-to-all-start
  164.9 0.0 copy-done.3
  164.9 0.0 copy-done.5
  164.9 0.6 convert_reduce_fusion
  165.6 285.6 %all-to-all-done = bf16[8,1280,1280]{2,1,0:T(8,128)(2,1)} async-done(((bf16[8,1280,1280]{2,1,0:T(8,128)(2,1)}), bf16[8,1280,1280]{2,1,0:T(8,128)(2,1)}, u32[]{:S(2)}, u32[]{:S(2)}) %all-to-all-start) | async-done | bytes 26214432 | tf_op jit(solution)/shard_map/all_to_all | solution.py:50
  451.2 0.0 copy-start.4
  451.2 598.5 %fusion.2.clone.4 = bf16[10240,5120]{1,0:T(8,128)(2,1)} fusion(bf16[10240,1280]{1,0:T(8,128)(2,1)} %bitcast.12, f32[5120]{0:T(1024)S(1)} %bitcast.73, bf16[1,1280,5120]{2,1,0:T(8,128)(2,1)} %param.16), kind=kOutput, calls=%fused_computation.8.clone.clone.clone.1 | convolution fusion | flops 137678028800 | bytes 144199680 | tf_op jit(solution)/shard_map/dot_general | solution.py:30
  1049.7 0.0 copy-done.4
  1049.7 0.0 copy-start.6
  1049.7 145.9 %add_convert_fusion = bf16[10240,1280]{1,0:T(8,128)(2,1)} fusion(f32[1280]{0:T(1024)S(1)} %copy-done.4, bf16[1,5120,1280]{2,1,0:T(8,128)(2,1)} %param.18, bf16[10240,5120]{1,0:T(8,128)(2,1)} %fusion.2.clone.4), kind=kOutput, calls=%fused_computation.24 | convolution fusion | flops 134243942400 | bytes 144184320 | tf_op jit(solution)/shard_map/dot_general | solution.py:32
  1195.6 0.0 copy-start.1
  1195.6 5.4 all-to-all-start.1
  1201.0 30.6 %scatter_custom_fusion = s32[8192]{0:T(1024)S(1)} fusion(s32[8192]{0:T(1024)} %bitcast.70, s32[8192]{0:T(1024)} %get-tuple-element.5, s32[]{:T(128)} %constant.42.clone.1), kind=kCustom, calls=%fused_computation.65 | custom fusion | bytes 33280 | tf_op jit(solution)/shard_map/scatter | solution.py:24
  1231.6 0.0 copy-done
  1231.6 12.2 multiply_reduce_fusion
  1243.8 0.0 copy-done.6
  1243.8 0.1 fusion.26
  1244.6 4.1 fusion.60
  1248.7 0.1 fusion.19
  1248.8 0.0 copy-done.1
  1248.8 0.1 select_reduce_fusion
  1249.0 237.2 %all-to-all-done.1 = bf16[8,1280,1280]{2,1,0:T(8,128)(2,1)} async-done(((bf16[8,1280,1280]{2,1,0:T(8,128)(2,1)}), bf16[8,1280,1280]{2,1,0:T(8,128)(2,1)}, u32[]{:S(2)}, u32[]{:S(2)}) %all-to-all-start.1) | async-done | bytes 26214432 | tf_op jit(solution)/shard_map/all_to_all | solution.py:52
  1486.2 56.2 %gather_fusion.2 = bf16[8192,1280]{1,0:T(8,128)(2,1)} fusion(bf16[10240,1280]{1,0:T(8,128)(2,1)} %bitcast.17, s32[8192]{0:T(1024)S(1)} %fusion.21), kind=kCustom, calls=%fused_computation.2 | custom fusion | bytes 41975808 | tf_op jit(solution)/shard_map/jit(_take)/gather | solution.py:37
  1542.4 19.3 %multiply_convert_fusion = bf16[1,8192,1280]{2,1,0:T(8,128)(2,1)} fusion(bf16[8192,1280]{1,0:T(8,128)(2,1)} %gather_fusion.2, f32[8192]{0:T(1024)S(1)} %select_reduce_fusion, pred[8192]{0:T(1024)(128)(4,1)S(1)} %compare_and_fusion.1), kind=kLoop, calls=%fused_computation.25 | loop fusion | flops 41943040 | bytes 41984000 | tf_op jit(solution)/shard_map/convert_element_type | solution.py:38
  (9 shorter events, 0.1 us)
Async XLA Ops:
  0.0 1231.6 %copy-start = (bf16[1280,256]{1,0:T(8,128)(2,1)S(1)}, bf16[1280,256]{1,0:T(8,128)(2,1)}, u32[]{:S(2)}) copy-start(bf16[1280,256]{1,0:T(8,128)(2,1)} %param.13) | copy-start | bytes 1966084
  0.9 0.6 copy-start.2
  141.2 23.7 %copy-start.3 = (bf16[1,5120]{1,0:T(2,128)(2,1)S(1)}, bf16[1,5120]{1,0:T(2,128)(2,1)}, u32[]{:S(2)}) copy-start(bf16[1,5120]{1,0:T(2,128)(2,1)} %param.17) | copy-start | bytes 30724
  141.2 23.8 %copy-start.5 = (bf16[1,1280]{1,0:T(2,128)(2,1)S(1)}, bf16[1,1280]{1,0:T(2,128)(2,1)}, u32[]{:S(2)}) copy-start(bf16[1,1280]{1,0:T(2,128)(2,1)} %param.19) | copy-start | bytes 7684
  159.7 291.5 %all-to-all-start = ((bf16[8,1280,1280]{2,1,0:T(8,128)(2,1)}), bf16[8,1280,1280]{2,1,0:T(8,128)(2,1)}, u32[]{:S(2)}, u32[]{:S(2)}) async-start(bf16[8,1280,1280]{2,1,0:T(8,128)(2,1)} %broadcast_select_fusion), calls=%async_computation | async-start | bytes 52428800 | tf_op jit(solution)/shard_map/all_to_all | solution.py:50
  451.2 598.5 %copy-start.4 = (f32[1280]{0:T(1024)S(1)}, f32[1280]{0:T(1024)}, u32[]{:S(2)}) copy-start(f32[1280]{0:T(1024)} %convert_reduce_fusion) | copy-start | bytes 15364
  1049.7 194.1 %copy-start.6 = (bf16[8,256]{1,0:T(8,128)(2,1)S(1)}, bf16[8,256]{1,0:T(8,128)(2,1)}, u32[]{:S(2)}) copy-start(bf16[8,256]{1,0:T(8,128)(2,1)} %param.14) | copy-start | bytes 12292
  1195.6 53.2 %copy-start.1 = (s32[1,8192]{1,0:T(1,128)S(1)}, s32[1,8192]{1,0:T(1,128)}, u32[]{:S(2)}) copy-start(s32[1,8192]{1,0:T(1,128)} %param.11) | copy-start | bytes 98308
  1195.6 290.5 %all-to-all-start.1 = ((bf16[8,1280,1280]{2,1,0:T(8,128)(2,1)}), bf16[8,1280,1280]{2,1,0:T(8,128)(2,1)}, u32[]{:S(2)}, u32[]{:S(2)}) async-start(bf16[8,1280,1280]{2,1,0:T(8,128)(2,1)} %bitcast.64), calls=%async_computation.1 | async-start | bytes 52428800 | tf_op jit(solution)/shard_map/all_to_all | solution.py:52
where the time goes:
time: 1570 us; the launch traced here: 1560 us
  matrix products  761 us (48%)
  waiting for transfers between devices  523 us (33%)
  local copies, waits for them, and re-layouts  221 us (14%)
  other arithmetic  45.8 us (3%)
    dot_general x1, matrix products, expert_local(): jnp.dot(slot_rows, w_first, preferred_element_type=jnp.float32)  598 us
    all_to_all x1, waiting for transfers between devices, device_step(): lax.all_to_all(send_rows.reshape(num_experts, capacity, model_width), EXP...  286 us
    all_to_all x1, waiting for transfers between devices, device_step(): lax.all_to_all(expert_rows.reshape(num_experts, capacity, model_width), E...  237 us
    dot_general x1, matrix products, expert_local(): jnp.dot(hidden, w_second, preferred_element_type=jnp.float32)  146 us
    gather x1, local copies, waits for them, and re-layouts, route_local(): jnp.take(tok_rows, slot_source, axis=0, mode='fill', fill_value=0)  65.1 us
    gather x1, local copies, waits for them, and re-layouts, combine_local(): picked = jnp.take(back_rows, dest_slot, axis=0, mode='fill', fill_value=0)  56.2 us
    gather x1, local copies, waits for them, and re-layouts, route_local(): ranked_ids = jnp.take(id_row, order_row)  37.4 us
  transfers between devices with their start and end apart: 2, of which 2 were waited for; matrix products, arithmetic and copies ran while one was open for 3% of the time, Pallas kernels for 0%

commit v1 on v0

v1 whole, which is shorter than its diff:
```python
import functools

import jax
import jax.numpy as jnp
from jax import lax
from jax.experimental import pallas as pl
from jax.experimental.pallas import tpu as pltpu
from jax.sharding import PartitionSpec as P

EXPERT_AXES = ("ep_b", "ep_a")
CHUNKS = 5
BLK = 256
GRP = 16
WIN = 64
MESH = pl.DeviceIdType.MESH
HID_TILE = 512


def onehot(mask):
    return jnp.where(mask, 1.0, 0.0)


def route_kernel(num_experts, capacity, order_ref, ids_ref, table_ref, code_ref, base_ref, passes_ref, total_ref, hot, keep):
    tok = order_ref.shape[1]
    blocks = tok // BLK
    rows = blocks * num_experts
    expert_col = lax.broadcasted_iota(jnp.int32, (num_experts, BLK), 0)
    lane = lax.broadcasted_iota(jnp.int32, (BLK, BLK), 1)
    sub = lax.broadcasted_iota(jnp.int32, (BLK, BLK), 0)
    before = onehot(sub < lane).astype(jnp.bfloat16)
    ri = lax.broadcasted_iota(jnp.int32, (rows, rows), 0)
    ci = lax.broadcasted_iota(jnp.int32, (rows, rows), 1)
    same_e = (ri % num_experts) == (ci % num_experts)
    earlier_block = onehot(same_e & (ci < ri)).astype(jnp.bfloat16)
    any_block = onehot(same_e).astype(jnp.bfloat16)
    hi_iota = lax.broadcasted_iota(jnp.int32, (tok // 128, BLK), 0)
    lo_iota = lax.broadcasted_iota(jnp.int32, (128, BLK), 0)

    def hi_lo(b):
        order = order_ref[:, b * BLK:(b + 1) * BLK]
        return onehot(hi_iota == (order >> 7)).astype(jnp.bfloat16), onehot(lo_iota == (order & 127))

    def counts(oh):
        count = jnp.sum(oh, axis=1, keepdims=True)
        wide = jnp.broadcast_to(count, (rows, 128)).astype(jnp.bfloat16)
        prior = jnp.dot(earlier_block, wide, preferred_element_type=jnp.float32)
        within = jnp.dot(oh.astype(jnp.bfloat16), before, preferred_element_type=jnp.float32)
        return count, wide, prior, within

    for b in range(blocks):
        hi, lo = hi_lo(b)
        picked = jnp.dot(table_ref[...], hi, preferred_element_type=jnp.float32)
        ranked = jnp.sum(picked * lo, axis=0, keepdims=True).astype(jnp.int32)
        hot[b * num_experts:(b + 1) * num_experts, :] = onehot(expert_col == ranked)
    oh = hot[...]
    _, _, prior, within = counts(oh)
    hot[...] = oh * onehot(within + prior[:, :1] < capacity)
    acc = jnp.zeros((tok // 128, 128), jnp.float32)
    for b in range(blocks):
        hi, lo = hi_lo(b)
        kept = jnp.sum(hot[b * num_experts:(b + 1) * num_experts, :], axis=0, keepdims=True)
        acc += lax.dot_general(hi * kept.astype(jnp.bfloat16), lo.astype(jnp.bfloat16), (((1,), (1,)), ((), ())), preferred_element_type=jnp.float32)
    keep[...] = acc
    for b in range(blocks):
        kept = jnp.concatenate([keep[2 * b:2 * b + 1, :], keep[2 * b + 1:2 * b + 2, :]], axis=1)
        ids = ids_ref[:, b * BLK:(b + 1) * BLK]
        hot[b * num_experts:(b + 1) * num_experts, :] = onehot(expert_col == ids) * onehot(kept > 0.5)
    oh = hot[...]
    count, wide, prior, within = counts(oh)
    total = jnp.dot(any_block, wide, preferred_element_type=jnp.float32)
    start = prior.astype(jnp.int32)
    base = start // GRP
    local = (start - base * GRP)[:, :1]
    within = within.astype(jnp.int32) + local
    expert_row = lax.broadcasted_iota(jnp.int32, (rows, BLK), 0) % num_experts
    code = (within // WIN) * (num_experts * WIN) + expert_row * WIN + within % WIN
    hot[...] = oh * (code + 1).astype(jnp.float32)
    for b in range(blocks):
        one = jnp.sum(hot[b * num_experts:(b + 1) * num_experts, :], axis=0, keepdims=True)
        code_ref[b:b + 1, :] = one.astype(jnp.int32) - 1
    need = (local + count.astype(jnp.int32) + (WIN - 1)) // WIN
    base_ref[...] = base
    passes_ref[...] = jnp.broadcast_to(jnp.where(count > 0.5, need, 0), (rows, 128))
    total_ref[...] = total[:num_experts].astype(jnp.int32)


def route(order_row, id_row, num_experts, capacity):
    tok = order_row.shape[0]
    blocks = tok // BLK
    rows = blocks * num_experts
    table = id_row.reshape(tok // 128, 128).T.astype(jnp.bfloat16)
    small = jax.ShapeDtypeStruct((rows, 128), jnp.int32)
    code, base, need, total = pl.pallas_call(
        functools.partial(route_kernel, num_experts, capacity),
        out_shape=(jax.ShapeDtypeStruct((blocks, BLK), jnp.int32), small, small, jax.ShapeDtypeStruct((num_experts, 128), jnp.int32)),
        scratch_shapes=[pltpu.VMEM((rows, BLK), jnp.float32), pltpu.VMEM((tok // 128, 128), jnp.float32)],
        name="route",
    )(order_row[None], id_row[None], table)
    passes = jnp.max(need[:, 0].reshape(blocks, num_experts), axis=1)
    return code, base[:, 0], passes, total[:, 0]


def dispatch_kernel(num_experts, base_ref, passes_ref, x_ref, code_ref, o_ref):
    b = pl.program_id(0)
    span = WIN // GRP

    @pl.when(b == 0)
    def _():
        o_ref[...] = jnp.zeros_like(o_ref)

    code = code_ref[pl.ds(b, 1), :]
    rows = lax.broadcasted_iota(jnp.int32, (num_experts * WIN, BLK), 0)

    def one_pass(p, carry):
        sel = onehot(rows == code - p * (num_experts * WIN)).astype(jnp.bfloat16)
        win = jnp.dot(sel, x_ref[...], preferred_element_type=jnp.float32).astype(jnp.bfloat16)
        win = win.reshape(num_experts, span, GRP, x_ref.shape[1])
        for e in range(num_experts):
            at = pl.ds(jnp.minimum(base_ref[b * num_experts + e] + p * span, o_ref.shape[1] - span), span)
            o_ref[e, at] += win[e]
        return carry

    lax.fori_loop(0, passes_ref[b], one_pass, 0)


def dispatch(tok_rows, code, base, passes, num_experts, slot_groups):
    tok, width = tok_rows.shape
    size = slot_groups + WIN // GRP
    shape = (num_experts, size, GRP, width)
    return pl.pallas_call(
        functools.partial(dispatch_kernel, num_experts),
        grid_spec=pltpu.PrefetchScalarGridSpec(
            num_scalar_prefetch=2,
            grid=(tok // BLK,),
            in_specs=[
                pl.BlockSpec((BLK, width), lambda i, *_: (i, 0)),
                pl.BlockSpec(code.shape, lambda i, *_: (0, 0)),
            ],
            out_specs=pl.BlockSpec(shape, lambda i, *_: (0, 0, 0, 0), pipeline_mode=pl.Buffered(1)),
        ),
        out_shape=jax.ShapeDtypeStruct(shape, jnp.bfloat16),
        compiler_params=pltpu.CompilerParams(vmem_limit_bytes=48 * 2**20),
        name="dispatch",
    )(base, passes, tok_rows, code)


def partner(d):
    row, col = lax.axis_index("ep_b"), lax.axis_index("ep_a")
    to_row = (row + d // 4) % 2
    to_col = ((col // 2 + (d // 2) % 2) % 2) * 2 + (col % 2 + d % 2) % 2
    return to_row * 4 + to_col, {"ep_b": to_row, "ep_a": to_col}


def exchange_kernel(num_experts, slot_groups, send, w1_hbm, b1_ref, w2_hbm, b2_ref, back, recv, staged, w1, w2, x, y, h, sem_w, sem_x, sem_y, out_s, out_r, ret_s, ret_r):
    cg = slot_groups // CHUNKS
    me, _ = partner(0)

    def to_expert(d, c):
        peer, where = partner(d)
        return pltpu.make_async_remote_copy(send.at[peer, pl.ds(c * cg, cg)], recv.at[d, pl.ds(c * cg, cg)], out_s.at[d, c], out_r.at[d, c], device_id=where, device_id_type=MESH)

    def to_owner(d, c):
        _, where = partner(d)
        return pltpu.make_async_remote_copy(staged.at[d, pl.ds(c * cg, cg)], back.at[me, pl.ds(c * cg, cg)], ret_s.at[d, c], ret_r.at[d, c], device_id=where, device_id_type=MESH)

    barrier = pltpu.get_barrier_semaphore()
    for d in range(1, num_experts):
        pl.semaphore_signal(barrier, inc=1, device_id=partner(d)[1], device_id_type=MESH)
    pl.semaphore_wait(barrier, num_experts - 1)

    far_first = (6, 7, 2, 3, 4, 5, 1)
    for c in range(CHUNKS):
        for d in far_first:
            to_expert(d, c).start()
    load1 = pltpu.make_async_copy(w1_hbm, w1, sem_w.at[0])
    load2 = pltpu.make_async_copy(w2_hbm, w2, sem_w.at[1])
    load1.start()
    load2.start()
    load1.wait()
    load2.wait()

    def step(i, carry):
        c, g = i // (num_experts // 2), i % (num_experts // 2)
        here = pl.ds(c * cg, cg)

        @pl.when(g == 0)
        def _():
            own = pltpu.make_async_copy(send.at[me, here], x.at[0], sem_x.at[0])
            own.start()
            own.wait()

        @pl.when(g != 0)
        def _():
            to_expert(2 * g, c).wait_recv()
            got = pltpu.make_async_copy(recv.at[2 * g, here], x.at[0], sem_x.at[0])
            got.start()
            got.wait()

        to_expert(2 * g + 1, c).wait_recv()
        got = pltpu.make_async_copy(recv.at[2 * g + 1, here], x.at[1], sem_x.at[1])
        got.start()
        got.wait()

        rows = x[...].reshape(2 * cg * GRP, x.shape[3])
        for j in range(w1.shape[1] // HID_TILE):
            cols = pl.ds(j * HID_TILE, HID_TILE)
            pre = jnp.dot(rows, w1[:, cols], preferred_element_type=jnp.float32) + b1_ref[:, cols].astype(jnp.float32)
            act = pre * 0.5 * (1.0 + lax.erf(pre * 0.7071067811865476))
            h[:, cols] = act.astype(jnp.bfloat16)
        hidden = h[...]
        for j in range(w2.shape[1] // 256):
            cols = pl.ds(j * 256, 256)
            res = jnp.dot(hidden, w2[:, cols], preferred_element_type=jnp.float32) + b2_ref[:, cols].astype(jnp.float32)
            y[:, :, :, cols] = res.astype(jnp.bfloat16).reshape(2, cg, GRP, 256)

        @pl.when(g == 0)
        def _():
            own = pltpu.make_async_copy(y.at[0], back.at[me, here], sem_y.at[0])
            own.start()
            own.wait()

        @pl.when(g != 0)
        def _():
            put = pltpu.make_async_copy(y.at[0], staged.at[2 * g, here], sem_y.at[0])
            put.start()
            put.wait()
            to_owner(2 * g, c).start()

        put = pltpu.make_async_copy(y.at[1], staged.at[2 * g + 1, here], sem_y.at[1])
        put.start()
        put.wait()
        to_owner(2 * g + 1, c).start()
        return carry

    lax.fori_loop(0, CHUNKS * num_experts // 2, step, 0)
    for c in range(CHUNKS):
        for d in range(1, num_experts):
            to_expert(d, c).wait_send()
            to_owner(d, c).wait()


def exchange(send, slot_groups, w_first, b_first, w_second, b_second):
    num_experts, _, _, width = send.shape
    hidden = w_first.shape[1]
    cg = slot_groups // CHUNKS
    land = jax.ShapeDtypeStruct((num_experts, slot_groups, GRP, width), jnp.bfloat16)
    back = jax.ShapeDtypeStruct(send.shape, jnp.bfloat16)
    sems = pltpu.SemaphoreType.DMA((num_experts, CHUNKS))
    hbm = pl.BlockSpec(memory_space=pl.ANY)
    vmem = pl.BlockSpec(memory_space=pltpu.VMEM)
    return pl.pallas_call(
        functools.partial(exchange_kernel, num_experts, slot_groups),
        out_shape=(back, land, land),
        in_specs=[hbm, hbm, vmem, hbm, vmem],
        out_specs=(hbm, hbm, hbm),
        scratch_shapes=[
            pltpu.VMEM((width, hidden), jnp.bfloat16),
            pltpu.VMEM((hidden, width), jnp.bfloat16),
            pltpu.VMEM((2, cg, GRP, width), jnp.bfloat16),
            pltpu.VMEM((2, cg, GRP, width), jnp.bfloat16),
            pltpu.VMEM((2 * cg * GRP, hidden), jnp.bfloat16),
            pltpu.SemaphoreType.DMA((2,)),
            pltpu.SemaphoreType.DMA((2,)),
            pltpu.SemaphoreType.DMA((2,)),
            sems, sems, sems, sems,
        ],
        compiler_params=pltpu.CompilerParams(collective_id=0, has_side_effects=True, vmem_limit_bytes=60 * 2**20),
        name="exchange",
    )(send, w_first, b_first[None], w_second, b_second[None])[0]


def combine_kernel(num_experts, base_ref, passes_ref, total_ref, back_ref, code_ref, gate_ref, o_ref):
    b = pl.program_id(0)
    span = WIN // GRP
    width = o_ref.shape[1]
    code = jnp.transpose(jnp.broadcast_to(code_ref[pl.ds(b, 1), :], (128, BLK)))
    cols = lax.broadcasted_iota(jnp.int32, (BLK, 128), 1)
    row = lax.broadcasted_iota(jnp.int32, (WIN, width), 0)
    gate = gate_ref[...]

    def picked(p):
        sel = jnp.concatenate([onehot(cols + k == code - p * (num_experts * WIN)) for k in range(0, num_experts * WIN, 128)], axis=1)
        wins = []
        for e in range(num_experts):
            at = jnp.minimum(base_ref[b * num_experts + e] + p * span, back_ref.shape[1] - span)
            win = back_ref[e, pl.ds(at, span)].reshape(WIN, width)
            wins.append(jnp.where(row < total_ref[e] - at * GRP, win, jnp.zeros_like(win)))
        return jnp.dot(sel.astype(jnp.bfloat16), jnp.concatenate(wins, axis=0), preferred_element_type=jnp.float32)

    o_ref[...] = (gate * picked(0)).astype(jnp.bfloat16)

    def more(p, carry):
        o_ref[...] += (gate * picked(p)).astype(jnp.bfloat16)
        return carry

    lax.fori_loop(1, passes_ref[b], more, 0)


def combine(back, code, base, passes, total, gate):
    tok, width = gate.shape[0], back.shape[3]
    num_experts = back.shape[0]
    return pl.pallas_call(
        functools.partial(combine_kernel, num_experts),
        grid_spec=pltpu.PrefetchScalarGridSpec(
            num_scalar_prefetch=3,
            grid=(tok // BLK,),
            in_specs=[
                pl.BlockSpec(back.shape, lambda i, *_: (0, 0, 0, 0), pipeline_mode=pl.Buffered(1)),
                pl.BlockSpec(code.shape, lambda i, *_: (0, 0)),
                pl.BlockSpec((BLK, 1), lambda i, *_: (i, 0)),
            ],
            out_specs=pl.BlockSpec((BLK, width), lambda i, *_: (i, 0)),
        ),
        out_shape=jax.ShapeDtypeStruct((tok, width), jnp.bfloat16),
        compiler_params=pltpu.CompilerParams(vmem_limit_bytes=48 * 2**20),
        name="combine",
    )(base, passes, total, back, code, gate)


def gates(tok_rows, id_row, w_route, expert_keys, tau):
    keys_f32 = expert_keys.astype(jnp.float32)
    key_unit = keys_f32 / jnp.sqrt(jnp.sum(keys_f32 * keys_f32, axis=1, keepdims=True))
    projected = jnp.dot(tok_rows, w_route, preferred_element_type=jnp.float32)
    proj_unit = projected / jnp.sqrt(jnp.sum(projected * projected, axis=1, keepdims=True))
    prob = jax.nn.softmax(jnp.dot(proj_unit, key_unit.T) / tau, axis=1)
    expert_range = jnp.arange(expert_keys.shape[0], dtype=jnp.int32)[None, :]
    return jnp.sum(jnp.where(id_row[:, None] == expert_range, prob, 0.0), axis=1, keepdims=True)


def solution(mesh):
    num_experts = mesh.shape["ep_b"] * mesh.shape["ep_a"]
    tok_spec = P(("dp",) + EXPERT_AXES)
    expert_spec = P(EXPERT_AXES)

    def device_step(tokens, expert_ids, route_order, w_route, expert_keys, tau, w_in, b_in, w_out, b_out):
        tok_rows, id_row = tokens[0], expert_ids[0]
        tok, width = tok_rows.shape
        capacity = (5 * tok + 4 * num_experts - 1) // (4 * num_experts)
        slot_groups = -(-capacity // (GRP * CHUNKS)) * CHUNKS
        code, base, passes, total = route(route_order[0], id_row, num_experts, capacity)
        send = dispatch(tok_rows, code, base, passes, num_experts, slot_groups)
        back = exchange(send, slot_groups, w_in[0], b_in[0], w_out[0], b_out[0])
        gate = gates(tok_rows, id_row, w_route, expert_keys, tau)
        return combine(back, code, base, passes, total, gate)[None]

    return jax.shard_map(
        device_step,
        mesh=mesh,
        in_specs=(tok_spec, tok_spec, tok_spec, P(), P(), P(), expert_spec, expert_spec, expert_spec, expert_spec),
        out_specs=tok_spec,
        check_vma=False,
    )
```

time: 1570 us -> 677 us (0.43)
  matrix products: 761 us -> 16.3 us
  Pallas kernels: 0 us -> 647 us
  waiting for transfers between devices: 523 us -> 0 us
  local copies, waits for them, and re-layouts: 221 us -> 8.36 us
  other arithmetic: 45.8 us -> 1.39 us
    dot_general x4 -> x2, matrix products: 761 us -> 16.3 us  [the longest x1 12.2 us: gates(): projected = jnp.dot(tok_rows, w_route, preferred_element_type=jnp.float32)]
    pallas_call x0 -> x4, Pallas kernels: none -> 647 us  [the longest x1 570 us: exchange(): pl.pallas_call(functools.partial(exchange_kernel, num_experts, slot_group...]
    all_to_all x2 -> x0, waiting for transfers between devices: 523 us -> none  [the longest x1 286 us: device_step(): lax.all_to_all(send_rows.reshape(num_experts, capacity, model_width), EXP...]
    gather x3 -> x0, local copies, waits for them, and re-layouts: 159 us -> none  [the longest x1 65.1 us: route_local(): jnp.take(tok_rows, slot_source, axis=0, mode='fill', fill_value=0)]
    scatter x2 -> x0, local copies, waits for them, and re-layouts: 61.3 us -> none  [the longest x1 30.7 us: route_local(): jnp.full((num_experts * capacity,), tok_dev, jnp.int32).at[ranked_slot]]
    select_n x6 -> x0, other arithmetic: 22.4 us -> none  [the longest x1 18.5 us: route_local(): jnp.take(tok_rows, slot_source, axis=0, mode='fill', fill_value=0)]
    convert_element_type x2 -> x1, other arithmetic: 19.3 us -> 0.91 us  [route(): table = id_row.reshape(tok // 128, 128).T.astype(jnp.bfloat16)]
  transfers between devices with their start and end apart: 2 -> 0, of which waited for: 2 -> 0; matrix products, arithmetic and copies ran while one was open for 3% -> 0% of each run, Pallas kernels for 0% -> 0%
where the time goes in v1:
time: 677 us; the launch traced here: 673 us
  Pallas kernels  647 us (96%)
  matrix products  16.3 us (2%)
  local copies, waits for them, and re-layouts  8.36 us (1%)
    pallas_call x1, Pallas kernels, exchange(): pl.pallas_call(functools.partial(exchange_kernel, num_experts, slot_group...  570 us
    pallas_call x1, Pallas kernels, dispatch(): pl.pallas_call(functools.partial(dispatch_kernel, num_experts), grid_spec...  39 us
    pallas_call x1, Pallas kernels, combine(): pl.pallas_call(functools.partial(combine_kernel, num_experts), grid_spec=...  32.7 us

profile of v1, /device:TPU:0, one launch (start us, length us, event | category | flops | bytes accessed | tf_op | source)
XLA Modules:
  0.0 673.5 jit_solution(7913427669688285703)
XLA Ops:
  0.0 0.0 copy-start
  0.0 0.9 convert_reduce_fusion
  0.9 0.7 copy.11
  1.6 4.9 route.1
  6.5 1.1 slice_reduce_fusion
  7.6 0.1 reshape_squeeze.4
  7.7 0.1 reduce_max.18.passes_ref
  7.9 0.8 slice_reduce_fusion.2.total_ref
  8.6 0.0 copy-start.3
  8.6 0.8 copy-done.3
  9.4 39.0 %dispatch.1.send = bf16[8,84,16,1280]{3,2,1,0:T(8,128)(2,1)} custom-call(s32[256]{0:T(256)S(1)} %get-tuple-element.20.base_ref, s32[32]{0:T(128)S(1)} %reduce_max.18.passes_ref, bf16[8192,1280]{1,0:T(8,128)(2,1)} %bitcast.13, s32[32,256]{1,0:T(8,128)S(1)} %copy-done.3), custom_call_target="tpu_custom_call" | custom-call | tf_op jit(solution)/shard_map/dispatch/pallas_call | solution.py:130
  48.4 0.0 copy-start.6
  48.4 570.2 %exchange.1 = (bf16[8,84,16,1280]{3,2,1,0:T(8,128)(2,1)}, bf16[8,80,16,1280]{3,2,1,0:T(8,128)(2,1)}, bf16[8,80,16,1280]{3,2,1,0:T(8,128)(2,1)}) custom-call(bf16[8,84,16,1280]{3,2,1,0:T(8,128)(2,1)} %dispatch.1.send, bf16[1280,5120]{1,0:T(8,128)(2,1)} %bitcast.14, bf16[1,5120]{1,0:T(2,128)(2,1)} %b1_ref.1, bf16[5120,1280]{1,0:T(8,128)(2,1)} %bitcast.15, ...), custom_call_target="tpu_custom_call" | custom-call | tf_op jit(solution)/shard_map/exchange/pallas_call | solution.py:251
  619.2 0.0 copy-done.6
  619.2 0.1 fusion.3
  619.3 0.0 copy-done
  619.3 12.2 %multiply_reduce_fusion = (f32[8192]{0:T(1024)S(1)}, f32[8192,256]{0,1:T(8,128)}) fusion(bf16[1280,256]{1,0:T(8,128)(2,1)S(1)} %copy-done, bf16[1,8192,1280]{2,1,0:T(8,128)(2,1)} %param.10), kind=kOutput, calls=%fused_computation.1 | convolution fusion | flops 5372895232 | bytes 30048256 | tf_op jit(solution)/shard_map/dot_general | solution.py:323
  631.5 0.0 copy-start.5
  631.5 0.0 copy-start.4
  631.6 4.1 fusion.7
  635.7 0.1 fusion.2
  635.8 0.0 copy-done.5
  635.8 0.1 select_reduce_fusion
  635.9 2.7 copy.12.gate_ref
  638.6 0.0 copy-done.4
  638.6 0.0 copy-start.2
  638.6 2.2 copy-done.2
  640.8 0.0 copy-start.1
  640.8 32.7 %combine.1 = bf16[8192,1280]{1,0:T(8,128)(2,1)} custom-call(s32[256]{0:T(256)S(1)} %get-tuple-element.20.base_ref, s32[32]{0:T(128)S(1)} %reduce_max.18.passes_ref, s32[8]{0:T(128)S(1)} %slice_reduce_fusion.2.total_ref, bf16[8,84,16,1280]{3,2,1,0:T(8,128)(2,1)} %get-tuple-element.14.back_ref, s32[32,256]{1,0:T(8,128)S(1)} %copy-done.4, f32[8192,1]{1,0:T(8,128)S(1)} %copy-done.2), custom_call_target="tpu_custom_call" | custom-call | tf_op jit(solution)/shard_map/combine/pallas_call | solution.py:302
  673.5 0.0 copy-done.1
  (2 shorter events, 0.0 us)
Async XLA Ops:
  0.0 619.3 %copy-start = (bf16[1280,256]{1,0:T(8,128)(2,1)S(1)}, bf16[1280,256]{1,0:T(8,128)(2,1)}, u32[]{:S(2)}) copy-start(bf16[1280,256]{1,0:T(8,128)(2,1)} %param.13) | copy-start | bytes 1966084
  8.6 0.8 copy-start.3
  48.4 570.8 %copy-start.6 = (bf16[8,256]{1,0:T(8,128)(2,1)S(1)}, bf16[8,256]{1,0:T(8,128)(2,1)}, u32[]{:S(2)}) copy-start(bf16[8,256]{1,0:T(8,128)(2,1)} %param.14) | copy-start | bytes 12292
  631.5 4.2 copy-start.5
  631.5 7.0 %copy-start.4 = (s32[32,256]{1,0:T(8,128)S(1)}, s32[32,256]{1,0:T(8,128)}, u32[]{:S(2)}) copy-start(s32[32,256]{1,0:T(8,128)} %get-tuple-element.13.code_ref) | copy-start | bytes 98308
  638.6 2.2 copy-start.2
  640.8 32.7 %copy-start.1 = (bf16[1280,256]{1,0:T(8,128)(2,1)S(1)}, bf16[1280,256]{1,0:T(8,128)(2,1)}, u32[]{:S(2)}) copy-start(bf16[1280,256]{1,0:T(8,128)(2,1)} %param.13) | copy-start | bytes 1966084

commit v2 on v1

--- a/solution.py
+++ b/solution.py
@@ -10,7 +10,9 @@
 EXPERT_AXES = ("ep_b", "ep_a")
 CHUNKS = 5
 BLK = 256
+STEP = 4
 GRP = 16
+UNIT = 8
 WIN = 64
 MESH = pl.DeviceIdType.MESH
 HID_TILE = 512
@@ -20,7 +22,7 @@
     return jnp.where(mask, 1.0, 0.0)
 
 
-def route_kernel(num_experts, capacity, order_ref, ids_ref, table_ref, code_ref, base_ref, passes_ref, total_ref, hot, keep):
+def route_kernel(num_experts, capacity, order_ref, ids_ref, grid_ref, code_ref, meta_ref, hot, keep):
     tok = order_ref.shape[1]
     blocks = tok // BLK
     rows = blocks * num_experts
@@ -47,9 +49,10 @@
         within = jnp.dot(oh.astype(jnp.bfloat16), before, preferred_element_type=jnp.float32)
         return count, wide, prior, within
 
+    table = jnp.transpose(grid_ref[...].astype(jnp.float32)).astype(jnp.bfloat16)
     for b in range(blocks):
         hi, lo = hi_lo(b)
-        picked = jnp.dot(table_ref[...], hi, preferred_element_type=jnp.float32)
+        picked = jnp.dot(table, hi, preferred_element_type=jnp.float32)
         ranked = jnp.sum(picked * lo, axis=0, keepdims=True).astype(jnp.int32)
         hot[b * num_experts:(b + 1) * num_experts, :] = onehot(expert_col == ranked)
     oh = hot[...]
@@ -78,70 +81,98 @@
     for b in range(blocks):
         one = jnp.sum(hot[b * num_experts:(b + 1) * num_experts, :], axis=0, keepdims=True)
         code_ref[b:b + 1, :] = one.astype(jnp.int32) - 1
-    need = (local + count.astype(jnp.int32) + (WIN - 1)) // WIN
-    base_ref[...] = base
-    passes_ref[...] = jnp.broadcast_to(jnp.where(count > 0.5, need, 0), (rows, 128))
-    total_ref[...] = total[:num_experts].astype(jnp.int32)
+    need = jnp.where(count > 0.5, (local + count.astype(jnp.int32) + (WIN - 1)) // WIN, 0)
+    for row, value in enumerate((base, need, total, local, local + count.astype(jnp.int32))):
+        wide = jnp.broadcast_to(value[:, :1], (rows, 128)).astype(jnp.float32)
+        meta_ref[row:row + 1, :] = jnp.transpose(wide)[:1].astype(jnp.int32)
 
 
 def route(order_row, id_row, num_experts, capacity):
     tok = order_row.shape[0]
     blocks = tok // BLK
     rows = blocks * num_experts
-    table = id_row.reshape(tok // 128, 128).T.astype(jnp.bfloat16)
-    small = jax.ShapeDtypeStruct((rows, 128), jnp.int32)
-    code, base, need, total = pl.pallas_call(
+    return pl.pallas_call(
         functools.partial(route_kernel, num_experts, capacity),
-        out_shape=(jax.ShapeDtypeStruct((blocks, BLK), jnp.int32), small, small, jax.ShapeDtypeStruct((num_experts, 128), jnp.int32)),
+        out_shape=(jax.ShapeDtypeStruct((blocks, BLK), jnp.int32), jax.ShapeDtypeStruct((8, rows), jnp.int32)),
         scratch_shapes=[pltpu.VMEM((rows, BLK), jnp.float32), pltpu.VMEM((tok // 128, 128), jnp.float32)],
         name="route",
-    )(order_row[None], id_row[None], table)
-    passes = jnp.max(need[:, 0].reshape(blocks, num_experts), axis=1)
-    return code, base[:, 0], passes, total[:, 0]
-
-
-def dispatch_kernel(num_experts, base_ref, passes_ref, x_ref, code_ref, o_ref):
-    b = pl.program_id(0)
+    )(order_row[None], id_row[None], id_row.reshape(tok // 128, 128))
+
+
+def most(meta_ref, b, num_experts):
+    n = meta_ref[1, b * num_experts]
+    for e in range(1, num_experts):
+        n = jnp.maximum(n, meta_ref[1, b * num_experts + e])
+    return n
+
+
+def used_units(meta_ref, e):
+    return (meta_ref[2, e] + (UNIT * GRP - 1)) // (UNIT * GRP)
+
+
+def dispatch_kernel(num_experts, meta_ref, x_ref, code_ref, o_ref, acc, sem):
+    i, last = pl.program_id(0), pl.num_programs(0) - 1
     span = WIN // GRP
-
-    @pl.when(b == 0)
+    rows = lax.broadcasted_iota(jnp.int32, (num_experts * WIN, BLK), 0)
+    sub = lax.broadcasted_iota(jnp.int32, (GRP, x_ref.shape[1]), 0)
+
+    def block(k, carry):
+        b = i * STEP + k
+        code = code_ref[pl.ds(b, 1), :]
+        x = x_ref[pl.ds(pl.multiple_of(k * BLK, BLK), BLK), :]
+
+        def one_pass(p, carry):
+            sel = onehot(rows == code - p * (num_experts * WIN)).astype(jnp.bfloat16)
+            win = jnp.dot(sel, x, preferred_element_type=jnp.float32).astype(jnp.bfloat16)
+            win = win.reshape(num_experts, span, GRP, x_ref.shape[1])
+            for e in range(num_experts):
+                at = jnp.minimum(meta_ref[0, b * num_experts + e] + p * span, acc.shape[1] - span)
+                old = jnp.where(p == 0, meta_ref[3, b * num_experts + e], 0)
+                acc[e, at] = jnp.where(sub < old, acc[e, at], win[e, 0])
+                acc[e, pl.ds(at + 1, span - 1)] = win[e, 1:]
+            return carry
+
+        return lax.fori_loop(0, most(meta_ref, b, num_experts), one_pass, carry)
+
+    lax.fori_loop(0, STEP, block, 0)
+
+    def unit(e, u):
+        part = pl.ds(u * UNIT, UNIT)
+        return pltpu.make_async_copy(acc.at[e, part], o_ref.at[e, part], sem.at[e, u])
+
+    here, nxt = i * STEP, jnp.minimum(i + 1, last) * STEP
+    for e in range(num_experts):
+        done = jnp.where(i == last, used_units(meta_ref, e), meta_ref[0, nxt * num_experts + e] // UNIT)
+        lax.fori_loop(meta_ref[0, here * num_experts + e] // UNIT, done, lambda u, c, e=e: (unit(e, u).start(), c)[1], 0)
+
+    @pl.when(i == last)
     def _():
-        o_ref[...] = jnp.zeros_like(o_ref)
-
-    code = code_ref[pl.ds(b, 1), :]
-    rows = lax.broadcasted_iota(jnp.int32, (num_experts * WIN, BLK), 0)
-
-    def one_pass(p, carry):
-        sel = onehot(rows == code - p * (num_experts * WIN)).astype(jnp.bfloat16)
-        win = jnp.dot(sel, x_ref[...], preferred_element_type=jnp.float32).astype(jnp.bfloat16)
-        win = win.reshape(num_experts, span, GRP, x_ref.shape[1])
         for e in range(num_experts):
-            at = pl.ds(jnp.minimum(base_ref[b * num_experts + e] + p * span, o_ref.shape[1] - span), span)
-            o_ref[e, at] += win[e]
-        return carry
-
-    lax.fori_loop(0, passes_ref[b], one_pass, 0)
-
-
-def dispatch(tok_rows, code, base, passes, num_experts, slot_groups):
+            lax.fori_loop(0, used_units(meta_ref, e), lambda u, c, e=e: (unit(e, u).wait(), c)[1], 0)
+
+
+def dispatch(tok_rows, code, meta, num_experts, slot_groups):
     tok, width = tok_rows.shape
-    size = slot_groups + WIN // GRP
-    shape = (num_experts, size, GRP, width)
+    padded = slot_groups + WIN // GRP
     return pl.pallas_call(
         functools.partial(dispatch_kernel, num_experts),
         grid_spec=pltpu.PrefetchScalarGridSpec(
-            num_scalar_prefetch=2,
-            grid=(tok // BLK,),
+            num_scalar_prefetch=1,
+            grid=(tok // (BLK * STEP),),
             in_specs=[
-                pl.BlockSpec((BLK, width), lambda i, *_: (i, 0)),
+                pl.BlockSpec((STEP * BLK, width), lambda i, *_: (i, 0)),
                 pl.BlockSpec(code.shape, lambda i, *_: (0, 0)),
             ],
-            out_specs=pl.BlockSpec(shape, lambda i, *_: (0, 0, 0, 0), pipeline_mode=pl.Buffered(1)),
+            out_specs=pl.BlockSpec(memory_space=pl.ANY),
+            scratch_shapes=[
+                pltpu.VMEM((num_experts, padded, GRP, width), jnp.bfloat16),
+                pltpu.SemaphoreType.DMA((num_experts, slot_groups // UNIT)),
+            ],
         ),
-        out_shape=jax.ShapeDtypeStruct(shape, jnp.bfloat16),
+        out_shape=jax.ShapeDtypeStruct((num_experts, slot_groups, GRP, width), jnp.bfloat16),
         compiler_params=pltpu.CompilerParams(vmem_limit_bytes=48 * 2**20),
         name="dispatch",
-    )(base, passes, tok_rows, code)
+    )(meta, tok_rows, code)
 
 
 def partner(d):
@@ -151,7 +182,7 @@
     return to_row * 4 + to_col, {"ep_b": to_row, "ep_a": to_col}
 
 
-def exchange_kernel(num_experts, slot_groups, send, w1_hbm, b1_ref, w2_hbm, b2_ref, back, recv, staged, w1, w2, x, y, h, sem_w, sem_x, sem_y, out_s, out_r, ret_s, ret_r):
+def exchange_kernel(num_experts, slot_groups, send, w1_hbm, b1_ref, w2_hbm, b2_ref, tokens, wr_ref, keys_ref, tau_ref, back, recv, staged, probs, w1, w2, x, y, h, prob, sem_w, sem_x, sem_y, out_s, out_r, ret_s, ret_r):
     cg = slot_groups // CHUNKS
     me, _ = partner(0)
 
@@ -233,32 +264,57 @@
         return carry
 
     lax.fori_loop(0, CHUNKS * num_experts // 2, step, 0)
+
+    keys = keys_ref[...].astype(jnp.float32)
+    unit_keys = keys / jnp.sqrt(jnp.sum(keys * keys, axis=1, keepdims=True))
+    unit_keys = jnp.concatenate([unit_keys, jnp.zeros((128 - num_experts, keys.shape[1]), jnp.float32)], axis=0)
+    real = lax.broadcasted_iota(jnp.int32, prob.shape, 1) < num_experts
+
+    def gate_step(i, carry):
+        for half in range(2):
+            got = pltpu.make_async_copy(tokens.at[pl.ds((2 * i + half) * cg, cg)], x.at[half], sem_x.at[half])
+            got.start()
+            got.wait()
+        proj = jnp.dot(x[...].reshape(prob.shape[0], x.shape[3]), wr_ref[...], preferred_element_type=jnp.float32)
+        unit = proj / jnp.sqrt(jnp.sum(proj * proj, axis=1, keepdims=True))
+        logits = lax.dot_general(unit, unit_keys, (((1,), (1,)), ((), ())), preferred_element_type=jnp.float32) / tau_ref[0, 0]
+        top = jnp.max(jnp.where(real, logits, -jnp.inf), axis=1, keepdims=True)
+        weight = jnp.where(real, jnp.exp(logits - top), 0.0)
+        prob[...] = weight / jnp.sum(weight, axis=1, keepdims=True)
+        put = pltpu.make_async_copy(prob, probs.at[pl.ds(i * prob.shape[0], prob.shape[0])], sem_y.at[0])
+        put.start()
+        put.wait()
+        return carry
+
+    lax.fori_loop(0, probs.shape[0] // prob.shape[0], gate_step, 0)
     for c in range(CHUNKS):
         for d in range(1, num_experts):
             to_expert(d, c).wait_send()
             to_owner(d, c).wait()
 
 
-def exchange(send, slot_groups, w_first, b_first, w_second, b_second):
-    num_experts, _, _, width = send.shape
+def exchange(send, w_first, b_first, w_second, b_second, tok_rows, w_route, expert_keys, tau):
+    num_experts, slot_groups, _, width = send.shape
+    tok = tok_rows.shape[0]
     hidden = w_first.shape[1]
     cg = slot_groups // CHUNKS
     land = jax.ShapeDtypeStruct((num_experts, slot_groups, GRP, width), jnp.bfloat16)
-    back = jax.ShapeDtypeStruct(send.shape, jnp.bfloat16)
+    probs = jax.ShapeDtypeStruct((tok, 128), jnp.float32)
     sems = pltpu.SemaphoreType.DMA((num_experts, CHUNKS))
     hbm = pl.BlockSpec(memory_space=pl.ANY)
     vmem = pl.BlockSpec(memory_space=pltpu.VMEM)
     return pl.pallas_call(
         functools.partial(exchange_kernel, num_experts, slot_groups),
-        out_shape=(back, land, land),
-        in_specs=[hbm, hbm, vmem, hbm, vmem],
-        out_specs=(hbm, hbm, hbm),
+        out_shape=(land, land, land, probs),
+        in_specs=[hbm, hbm, vmem, hbm, vmem, hbm, vmem, vmem, pl.BlockSpec(memory_space=pltpu.SMEM)],
+        out_specs=(hbm, hbm, hbm, hbm),
         scratch_shapes=[
             pltpu.VMEM((width, hidden), jnp.bfloat16),
             pltpu.VMEM((hidden, width), jnp.bfloat16),
             pltpu.VMEM((2, cg, GRP, width), jnp.bfloat16),
             pltpu.VMEM((2, cg, GRP, width), jnp.bfloat16),
             pltpu.VMEM((2 * cg * GRP, hidden), jnp.bfloat16),
+            pltpu.VMEM((2 * cg * GRP, 128), jnp.float32),
             pltpu.SemaphoreType.DMA((2,)),
             pltpu.SemaphoreType.DMA((2,)),
             pltpu.SemaphoreType.DMA((2,)),
@@ -266,65 +322,87 @@
         ],
         compiler_params=pltpu.CompilerParams(collective_id=0, has_side_effects=True, vmem_limit_bytes=60 * 2**20),
         name="exchange",
-    )(send, w_first, b_first[None], w_second, b_second[None])[0]
-
-
-def combine_kernel(num_experts, base_ref, passes_ref, total_ref, back_ref, code_ref, gate_ref, o_ref):
-    b = pl.program_id(0)
+    )(send, w_first, b_first[None], w_second, b_second[None], tok_rows.reshape(tok // GRP, GRP, width), w_route, expert_keys, tau.reshape(1, 1))
+
+
+def combine_kernel(num_experts, meta_ref, back_ref, code_ref, prob_ref, o_ref, rows_in, sem):
+    i, last = pl.program_id(0), pl.num_programs(0) - 1
     span = WIN // GRP
     width = o_ref.shape[1]
-    code = jnp.transpose(jnp.broadcast_to(code_ref[pl.ds(b, 1), :], (128, BLK)))
     cols = lax.broadcasted_iota(jnp.int32, (BLK, 128), 1)
     row = lax.broadcasted_iota(jnp.int32, (WIN, width), 0)
-    gate = gate_ref[...]
-
-    def picked(p):
-        sel = jnp.concatenate([onehot(cols + k == code - p * (num_experts * WIN)) for k in range(0, num_experts * WIN, 128)], axis=1)
-        wins = []
-        for e in range(num_experts):
-            at = jnp.minimum(base_ref[b * num_experts + e] + p * span, back_ref.shape[1] - span)
-            win = back_ref[e, pl.ds(at, span)].reshape(WIN, width)
-            wins.append(jnp.where(row < total_ref[e] - at * GRP, win, jnp.zeros_like(win)))
-        return jnp.dot(sel.astype(jnp.bfloat16), jnp.concatenate(wins, axis=0), preferred_element_type=jnp.float32)
-
-    o_ref[...] = (gate * picked(0)).astype(jnp.bfloat16)
-
-    def more(p, carry):
-        o_ref[...] += (gate * picked(p)).astype(jnp.bfloat16)
-        return carry
-
-    lax.fori_loop(1, passes_ref[b], more, 0)
-
-
-def combine(back, code, base, passes, total, gate):
-    tok, width = gate.shape[0], back.shape[3]
-    num_experts = back.shape[0]
+
+    def unit(e, u):
+        part = pl.ds(u * UNIT, UNIT)
+        return pltpu.make_async_copy(back_ref.at[e, part], rows_in.at[e, part], sem.at[e, u])
+
+    @pl.when(i == 0)
+    def _():
+        for u in range(back_ref.shape[1] // UNIT):
+            for e in range(num_experts):
+                @pl.when(u < used_units(meta_ref, e))
+                def _():
+                    unit(e, u).start()
+
+    def reach(step, e):
+        n = (meta_ref[0, step * STEP * num_experts + e] * GRP + meta_ref[3, step * STEP * num_experts + e] + (UNIT * GRP - 1)) // (UNIT * GRP)
+        return n
+
+    for e in range(num_experts):
+        end = jnp.where(i == last, used_units(meta_ref, e), reach(jnp.minimum(i + 1, last), e))
+        lax.fori_loop(reach(i, e), end, lambda u, c, e=e: (unit(e, u).wait(), c)[1], 0)
+
+    def block(k, carry):
+        b = i * STEP + k
+        mine = pl.ds(pl.multiple_of(k * BLK, BLK), BLK)
+        code = jnp.transpose(jnp.broadcast_to(code_ref[pl.ds(b, 1), :], (128, BLK)))
+        expert = (code & (num_experts * WIN - 1)) // WIN
+        gate = jnp.sum(jnp.where(cols == expert, prob_ref[mine, :], 0.0), axis=1, keepdims=True)
+
+        def picked(p):
+            sel = jnp.concatenate([onehot(cols + k == code - p * (num_experts * WIN)) for k in range(0, num_experts * WIN, 128)], axis=1)
+            wins = []
+            for e in range(num_experts):
+                at = jnp.minimum(meta_ref[0, b * num_experts + e] + p * span, rows_in.shape[1] - span)
+                rows = rows_in[e, pl.ds(at, span)].reshape(WIN, width)
+                end = meta_ref[0, b * num_experts + e] * GRP + meta_ref[4, b * num_experts + e]
+                wins.append(jnp.where(row < end - at * GRP, rows, jnp.zeros_like(rows)))
+            return jnp.dot(sel.astype(jnp.bfloat16), jnp.concatenate(wins, axis=0), preferred_element_type=jnp.float32)
+
+        o_ref[mine, :] = (gate * picked(0)).astype(jnp.bfloat16)
+
+        def more(p, carry):
+            o_ref[mine, :] += (gate * picked(p)).astype(jnp.bfloat16)
+            return carry
+
+        return lax.fori_loop(1, most(meta_ref, b, num_experts), more, carry)
+
+    lax.fori_loop(0, STEP, block, 0)
+
+
+def combine(back, code, meta, probs):
+    tok, width = probs.shape[0], back.shape[3]
+    num_experts, slot_groups = back.shape[:2]
     return pl.pallas_call(
         functools.partial(combine_kernel, num_experts),
         grid_spec=pltpu.PrefetchScalarGridSpec(
-            num_scalar_prefetch=3,
-            grid=(tok // BLK,),
+            num_scalar_prefetch=1,
+            grid=(tok // (BLK * STEP),),
             in_specs=[
-                pl.BlockSpec(back.shape, lambda i, *_: (0, 0, 0, 0), pipeline_mode=pl.Buffered(1)),
+                pl.BlockSpec(memory_space=pl.ANY),
                 pl.BlockSpec(code.shape, lambda i, *_: (0, 0)),
-                pl.BlockSpec((BLK, 1), lambda i, *_: (i, 0)),
+                pl.BlockSpec((STEP * BLK, 128), lambda i, *_: (i, 0)),
             ],
-            out_specs=pl.BlockSpec((BLK, width), lambda i, *_: (i, 0)),
+            out_specs=pl.BlockSpec((STEP * BLK, width), lambda i, *_: (i, 0)),
+            scratch_shapes=[
+                pltpu.VMEM((num_experts, slot_groups + WIN // GRP, GRP, width), jnp.bfloat16),
+                pltpu.SemaphoreType.DMA((num_experts, slot_groups // UNIT)),
+            ],
         ),
         out_shape=jax.ShapeDtypeStruct((tok, width), jnp.bfloat16),
-        compiler_params=pltpu.CompilerParams(vmem_limit_bytes=48 * 2**20),
+        compiler_params=pltpu.CompilerParams(vmem_limit_bytes=56 * 2**20),
         name="combine",
-    )(base, passes, total, back, code, gate)
-
-
-def gates(tok_rows, id_row, w_route, expert_keys, tau):
-    keys_f32 = expert_keys.astype(jnp.float32)
-    key_unit = keys_f32 / jnp.sqrt(jnp.sum(keys_f32 * keys_f32, axis=1, keepdims=True))
-    projected = jnp.dot(tok_rows, w_route, preferred_element_type=jnp.float32)
-    proj_unit = projected / jnp.sqrt(jnp.sum(projected * projected, axis=1, keepdims=True))
-    prob = jax.nn.softmax(jnp.dot(proj_unit, key_unit.T) / tau, axis=1)
-    expert_range = jnp.arange(expert_keys.shape[0], dtype=jnp.int32)[None, :]
-    return jnp.sum(jnp.where(id_row[:, None] == expert_range, prob, 0.0), axis=1, keepdims=True)
+    )(meta, back, code, probs)
 
 
 def solution(mesh):
@@ -337,11 +415,10 @@
         tok, width = tok_rows.shape
         capacity = (5 * tok + 4 * num_experts - 1) // (4 * num_experts)
         slot_groups = -(-capacity // (GRP * CHUNKS)) * CHUNKS
-        code, base, passes, total = route(route_order[0], id_row, num_experts, capacity)
-        send = dispatch(tok_rows, code, base, passes, num_experts, slot_groups)
-        back = exchange(send, slot_groups, w_in[0], b_in[0], w_out[0], b_out[0])
-        gate = gates(tok_rows, id_row, w_route, expert_keys, tau)
-        return combine(back, code, base, passes, total, gate)[None]
+        code, meta = route(route_order[0], id_row, num_experts, capacity)
+        send = dispatch(tok_rows, code, meta, num_experts, slot_groups)
+        back, _, _, probs = exchange(send, w_in[0], b_in[0], w_out[0], b_out[0], tok_rows, w_route, expert_keys, tau)
+        return combine(back, code, meta, probs)[None]
 
     return jax.shard_map(
         device_step,

time: 677 us -> 638 us (0.942)
  matrix products: 16.3 us -> 0 us
  Pallas kernels: 647 us -> 632 us
  local copies, waits for them, and re-layouts: 8.36 us -> 1.45 us
    dot_general x2 -> x0, matrix products: 16.3 us -> none  [the longest x1 12.2 us: gates(): projected = jnp.dot(tok_rows, w_route, preferred_element_type=jnp.float32)]
    pallas_call x1, Pallas kernels: 39 us -> 25.8 us  [dispatch(): pl.pallas_call(functools.partial(dispatch_kernel, num_experts), grid_spec...]
where the time goes in v2:
time: 638 us; the launch traced here: 634 us
  Pallas kernels  632 us (99%)
    pallas_call x1, Pallas kernels, exchange(): pl.pallas_call(functools.partial(exchange_kernel, num_experts, slot_group...  572 us
    pallas_call x1, Pallas kernels, combine(): pl.pallas_call(functools.partial(combine_kernel, num_experts), grid_spec=...  28.8 us
    pallas_call x1, Pallas kernels, dispatch(): pl.pallas_call(functools.partial(dispatch_kernel, num_experts), grid_spec...  25.8 us

profile of v2, /device:TPU:0, one launch (start us, length us, event | category | flops | bytes accessed | tf_op | source)
XLA Modules:
  0.0 634.3 jit_solution(9210969924191094359)
XLA Ops:
  0.7 5.3 route.1
  6.0 0.0 copy-start
  6.0 0.8 copy-done
  6.8 0.0 copy-start.1
  6.8 0.7 copy-done.1
  7.4 25.8 %dispatch.1.send = bf16[8,80,16,1280]{3,2,1,0:T(8,128)(2,1)} custom-call(s32[8,256]{1,0:T(8,128)S(1)} %copy-done.1, bf16[8192,1280]{1,0:T(8,128)(2,1)} %bitcast.8, s32[32,256]{1,0:T(8,128)S(1)} %copy-done), custom_call_target="tpu_custom_call" | custom-call | tf_op jit(solution)/shard_map/dispatch/pallas_call | solution.py:157
  33.3 572.1 %exchange.1 = (bf16[8,80,16,1280]{3,2,1,0:T(8,128)(2,1)}, bf16[8,80,16,1280]{3,2,1,0:T(8,128)(2,1)}, bf16[8,80,16,1280]{3,2,1,0:T(8,128)(2,1)}, f32[8192,128]{1,0:T(8,128)}) custom-call(bf16[8,80,16,1280]{3,2,1,0:T(8,128)(2,1)} %dispatch.1.send, bf16[1280,5120]{1,0:T(8,128)(2,1)} %bitcast.10, bf16[1,5120]{1,0:T(2,128)(2,1)} %b1_ref.1, ...), custom_call_target="tpu_custom_call" | custom-call | tf_op jit(solution)/shard_map/exchange/pallas_call | solution.py:306
  605.3 28.8 %combine.1 = bf16[8192,1280]{1,0:T(8,128)(2,1)} custom-call(s32[8,256]{1,0:T(8,128)} %get-tuple-element.9.meta_ref, bf16[8,80,16,1280]{3,2,1,0:T(8,128)(2,1)} %get-tuple-element.11.back_ref, s32[32,256]{1,0:T(8,128)} %get-tuple-element.10.code_ref, f32[8192,128]{1,0:T(8,128)} %get-tuple-element.12.prob_ref), custom_call_target="tpu_custom_call" | custom-call | tf_op jit(solution)/shard_map/combine/pallas_call | solution.py:386
Async XLA Ops:
  6.0 0.8 copy-start
  6.8 0.7 copy-start.1

commit v3 on v2

--- a/solution.py
+++ b/solution.py
@@ -82,6 +82,16 @@
         one = jnp.sum(hot[b * num_experts:(b + 1) * num_experts, :], axis=0, keepdims=True)
         code_ref[b:b + 1, :] = one.astype(jnp.int32) - 1
     need = jnp.where(count > 0.5, (local + count.astype(jnp.int32) + (WIN - 1)) // WIN, 0)
+    early = jnp.zeros((1, 1), jnp.float32)
+    ahead = onehot(start[:, :1] <= (capacity - UNIT * GRP) // (UNIT * GRP) * (UNIT * GRP))
+    for b in range(STEP, blocks, STEP):
+        early += jnp.min(ahead[b * num_experts:(b + 1) * num_experts], axis=0, keepdims=True)
+    needed = jnp.ones((1, 1), jnp.float32)
+    behind = onehot(start[:, :1] < UNIT * GRP)
+    for b in range(1, blocks):
+        needed += jnp.max(behind[b * num_experts:(b + 1) * num_experts], axis=0, keepdims=True)
+    meta_ref[6:7, :] = jnp.broadcast_to(needed, (1, rows)).astype(jnp.int32)
+    meta_ref[5:6, :] = jnp.broadcast_to(early, (1, rows)).astype(jnp.int32)
     for row, value in enumerate((base, need, total, local, local + count.astype(jnp.int32))):
         wide = jnp.broadcast_to(value[:, :1], (rows, 128)).astype(jnp.float32)
         meta_ref[row:row + 1, :] = jnp.transpose(wide)[:1].astype(jnp.int32)
@@ -110,29 +120,83 @@
     return (meta_ref[2, e] + (UNIT * GRP - 1)) // (UNIT * GRP)
 
 
-def dispatch_kernel(num_experts, meta_ref, x_ref, code_ref, o_ref, acc, sem):
+def place(num_experts, meta_ref, b, code, x, acc):
+    span = WIN // GRP
+    width = x.shape[1]
+    rows = lax.broadcasted_iota(jnp.int32, (num_experts * WIN, BLK), 0)
+    sub = lax.broadcasted_iota(jnp.int32, (GRP, width), 0)
+
+    def one_pass(p, carry):
+        sel = onehot(rows == code - p * (num_experts * WIN)).astype(jnp.bfloat16)
+        win = jnp.dot(sel, x, preferred_element_type=jnp.float32).astype(jnp.bfloat16)
+        win = win.reshape(num_experts, span, GRP, width)
+        for e in range(num_experts):
+            at = jnp.minimum(meta_ref[0, b * num_experts + e] + p * span, acc.shape[1] - span)
+            old = jnp.where(p == 0, meta_ref[3, b * num_experts + e], 0)
+            acc[e, at] = jnp.where(sub < old, acc[e, at], win[e, 0])
+            acc[e, pl.ds(at + 1, span - 1)] = win[e, 1:]
+        return carry
+
+    lax.fori_loop(0, most(meta_ref, b, num_experts), one_pass, 0)
+
+
+def first_kernel(num_experts, meta_ref, x_ref, code_ref, o_ref, acc, ring, sem_x, sem_o):
+    blocks = meta_ref[6, 0]
+    depth = ring.shape[0]
+
+    def load(b):
+        return pltpu.make_async_copy(x_ref.at[pl.ds(pl.multiple_of(b * BLK, BLK), BLK)], ring.at[b % depth], sem_x.at[b % depth])
+
+    for b in range(depth):
+        @pl.when(b < blocks)
+        def _():
+            load(b).start()
+
+    def block(b, carry):
+        load(b).wait()
+        place(num_experts, meta_ref, b, code_ref[pl.ds(b, 1), :], ring[b % depth], acc)
+
+        @pl.when(b + depth < blocks)
+        def _():
+            load(b + depth).start()
+
+        return carry
+
+    lax.fori_loop(0, blocks, block, 0)
+    outs = [pltpu.make_async_copy(acc.at[e, pl.ds(0, UNIT)], o_ref.at[e], sem_o.at[e]) for e in range(num_experts)]
+    for out in outs:
+        out.start()
+    for out in outs:
+        out.wait()
+
+
+def dispatch_first(tok_rows, code, meta, num_experts):
+    width = tok_rows.shape[1]
+    depth = 8
+    return pl.pallas_call(
+        functools.partial(first_kernel, num_experts),
+        in_specs=[pl.BlockSpec(memory_space=pltpu.SMEM), pl.BlockSpec(memory_space=pl.ANY), pl.BlockSpec(memory_space=pltpu.VMEM)],
+        out_specs=pl.BlockSpec(memory_space=pl.ANY),
+        out_shape=jax.ShapeDtypeStruct((num_experts, UNIT, GRP, width), jnp.bfloat16),
+        scratch_shapes=[
+            pltpu.VMEM((num_experts, UNIT + WIN // GRP, GRP, width), jnp.bfloat16),
+            pltpu.VMEM((depth, BLK, width), jnp.bfloat16),
+            pltpu.SemaphoreType.DMA((depth,)),
+            pltpu.SemaphoreType.DMA((num_experts,)),
+        ],
+        compiler_params=pltpu.CompilerParams(vmem_limit_bytes=32 * 2**20),
+        name="dispatch_first",
+    )(meta, tok_rows, code)
+
+
+def dispatch_kernel(num_experts, meta_ref, x_ref, code_ref, _, o_ref, acc, sem):
     i, last = pl.program_id(0), pl.num_programs(0) - 1
-    span = WIN // GRP
-    rows = lax.broadcasted_iota(jnp.int32, (num_experts * WIN, BLK), 0)
-    sub = lax.broadcasted_iota(jnp.int32, (GRP, x_ref.shape[1]), 0)
 
     def block(k, carry):
         b = i * STEP + k
-        code = code_ref[pl.ds(b, 1), :]
         x = x_ref[pl.ds(pl.multiple_of(k * BLK, BLK), BLK), :]
-
-        def one_pass(p, carry):
-            sel = onehot(rows == code - p * (num_experts * WIN)).astype(jnp.bfloat16)
-            win = jnp.dot(sel, x, preferred_element_type=jnp.float32).astype(jnp.bfloat16)
-            win = win.reshape(num_experts, span, GRP, x_ref.shape[1])
-            for e in range(num_experts):
-                at = jnp.minimum(meta_ref[0, b * num_experts + e] + p * span, acc.shape[1] - span)
-                old = jnp.where(p == 0, meta_ref[3, b * num_experts + e], 0)
-                acc[e, at] = jnp.where(sub < old, acc[e, at], win[e, 0])
-                acc[e, pl.ds(at + 1, span - 1)] = win[e, 1:]
-            return carry
-
-        return lax.fori_loop(0, most(meta_ref, b, num_experts), one_pass, carry)
+        place(num_experts, meta_ref, b, code_ref[pl.ds(b, 1), :], x, acc)
+        return carry
 
     lax.fori_loop(0, STEP, block, 0)
 
@@ -142,17 +206,19 @@
 
     here, nxt = i * STEP, jnp.minimum(i + 1, last) * STEP
     for e in range(num_experts):
+        begin = jnp.maximum(meta_ref[0, here * num_experts + e] // UNIT, 1)
         done = jnp.where(i == last, used_units(meta_ref, e), meta_ref[0, nxt * num_experts + e] // UNIT)
-        lax.fori_loop(meta_ref[0, here * num_experts + e] // UNIT, done, lambda u, c, e=e: (unit(e, u).start(), c)[1], 0)
+        lax.fori_loop(begin, done, lambda u, c, e=e: (unit(e, u).start(), c)[1], 0)
 
     @pl.when(i == last)
     def _():
         for e in range(num_experts):
-            lax.fori_loop(0, used_units(meta_ref, e), lambda u, c, e=e: (unit(e, u).wait(), c)[1], 0)
-
-
-def dispatch(tok_rows, code, meta, num_experts, slot_groups):
+            lax.fori_loop(1, used_units(meta_ref, e), lambda u, c, e=e: (unit(e, u).wait(), c)[1], 0)
+
+
+def dispatch(tok_rows, code, meta, first, slot_groups):
     tok, width = tok_rows.shape
+    num_experts = first.shape[0]
     padded = slot_groups + WIN // GRP
     return pl.pallas_call(
         functools.partial(dispatch_kernel, num_experts),
@@ -162,6 +228,7 @@
             in_specs=[
                 pl.BlockSpec((STEP * BLK, width), lambda i, *_: (i, 0)),
                 pl.BlockSpec(code.shape, lambda i, *_: (0, 0)),
+                pl.BlockSpec(memory_space=pl.ANY),
             ],
             out_specs=pl.BlockSpec(memory_space=pl.ANY),
             scratch_shapes=[
@@ -171,8 +238,9 @@
         ),
         out_shape=jax.ShapeDtypeStruct((num_experts, slot_groups, GRP, width), jnp.bfloat16),
         compiler_params=pltpu.CompilerParams(vmem_limit_bytes=48 * 2**20),
+        cost_estimate=pl.CostEstimate(flops=2 * tok * num_experts * WIN * width, bytes_accessed=5 * tok * width, transcendentals=0),
         name="dispatch",
-    )(meta, tok_rows, code)
+    )(meta, tok_rows, code, first)
 
 
 def partner(d):
@@ -182,17 +250,20 @@
     return to_row * 4 + to_col, {"ep_b": to_row, "ep_a": to_col}
 
 
-def exchange_kernel(num_experts, slot_groups, send, w1_hbm, b1_ref, w2_hbm, b2_ref, tokens, wr_ref, keys_ref, tau_ref, back, recv, staged, probs, w1, w2, x, y, h, prob, sem_w, sem_x, sem_y, out_s, out_r, ret_s, ret_r):
+def exchange_kernel(num_experts, slot_groups, first, send, w1_hbm, b1_ref, w2_hbm, b2_ref, tokens, wr_ref, keys_ref, tau_ref, back, recv, staged, tail, probs, w1, w2, x, y, h, prob, sem_w, sem_x, sem_y, out_s, out_r, ret_s, ret_r):
     cg = slot_groups // CHUNKS
+    units = slot_groups // UNIT
     me, _ = partner(0)
 
-    def to_expert(d, c):
+    def to_expert(d, u):
         peer, where = partner(d)
-        return pltpu.make_async_remote_copy(send.at[peer, pl.ds(c * cg, cg)], recv.at[d, pl.ds(c * cg, cg)], out_s.at[d, c], out_r.at[d, c], device_id=where, device_id_type=MESH)
-
-    def to_owner(d, c):
+        part = pl.ds(u * UNIT, UNIT)
+        return pltpu.make_async_remote_copy(send.at[peer, part], recv.at[d, part], out_s.at[d, u], out_r.at[d, u], device_id=where, device_id_type=MESH)
+
+    def to_owner(d, u):
         _, where = partner(d)
-        return pltpu.make_async_remote_copy(staged.at[d, pl.ds(c * cg, cg)], back.at[me, pl.ds(c * cg, cg)], ret_s.at[d, c], ret_r.at[d, c], device_id=where, device_id_type=MESH)
+        part = pl.ds(u * UNIT, UNIT)
+        return pltpu.make_async_remote_copy(staged.at[d, part], back.at[me, part], ret_s.at[d, u], ret_r.at[d, u], device_id=where, device_id_type=MESH)
 
     barrier = pltpu.get_barrier_semaphore()
     for d in range(1, num_experts):
@@ -200,9 +271,9 @@
     pl.semaphore_wait(barrier, num_experts - 1)
 
     far_first = (6, 7, 2, 3, 4, 5, 1)
-    for c in range(CHUNKS):
+    for u in range(1, units):
         for d in far_first:
-            to_expert(d, c).start()
+            to_expert(d, u).start()
     load1 = pltpu.make_async_copy(w1_hbm, w1, sem_w.at[0])
     load2 = pltpu.make_async_copy(w2_hbm, w2, sem_w.at[1])
     load1.start()
@@ -212,25 +283,32 @@
 
     def step(i, carry):
         c, g = i // (num_experts // 2), i % (num_experts // 2)
-        here = pl.ds(c * cg, cg)
-
-        @pl.when(g == 0)
-        def _():
-            own = pltpu.make_async_copy(send.at[me, here], x.at[0], sem_x.at[0])
-            own.start()
-            own.wait()
-
-        @pl.when(g != 0)
-        def _():
-            to_expert(2 * g, c).wait_recv()
-            got = pltpu.make_async_copy(recv.at[2 * g, here], x.at[0], sem_x.at[0])
-            got.start()
-            got.wait()
-
-        to_expert(2 * g + 1, c).wait_recv()
-        got = pltpu.make_async_copy(recv.at[2 * g + 1, here], x.at[1], sem_x.at[1])
-        got.start()
-        got.wait()
+        per = cg // UNIT
+
+        def take(src, half, k):
+            return pltpu.make_async_copy(src, x.at[half, pl.ds(k * UNIT, UNIT)], sem_x.at[half, k])
+
+        for half in range(2):
+            d = 2 * g + half
+            for k in range(per):
+                u = c * per + k
+                part = pl.ds(u * UNIT, UNIT)
+
+                @pl.when(u == 0)
+                def _():
+                    take(first.at[partner(d)[0]], half, k).start()
+
+                @pl.when((u != 0) & (d == 0))
+                def _():
+                    take(send.at[me, part], half, k).start()
+
+                @pl.when((u != 0) & (d != 0))
+                def _():
+                    to_expert(d, u).wait_recv()
+                    take(recv.at[d, part], half, k).start()
+        for half in range(2):
+            for k in range(per):
+                take(first.at[me], half, k).wait()
 
         rows = x[...].reshape(2 * cg * GRP, x.shape[3])
         for j in range(w1.shape[1] // HID_TILE):
@@ -244,23 +322,36 @@
             res = jnp.dot(hidden, w2[:, cols], preferred_element_type=jnp.float32) + b2_ref[:, cols].astype(jnp.float32)
             y[:, :, :, cols] = res.astype(jnp.bfloat16).reshape(2, cg, GRP, 256)
 
-        @pl.when(g == 0)
-        def _():
-            own = pltpu.make_async_copy(y.at[0], back.at[me, here], sem_y.at[0])
-            own.start()
-            own.wait()
-
-        @pl.when(g != 0)
-        def _():
-            put = pltpu.make_async_copy(y.at[0], staged.at[2 * g, here], sem_y.at[0])
-            put.start()
-            put.wait()
-            to_owner(2 * g, c).start()
-
-        put = pltpu.make_async_copy(y.at[1], staged.at[2 * g + 1, here], sem_y.at[1])
-        put.start()
-        put.wait()
-        to_owner(2 * g + 1, c).start()
+        def put(half, k, dst):
+            return pltpu.make_async_copy(y.at[half, pl.ds(k * UNIT, UNIT)], dst, sem_y.at[half, k])
+
+        for half in range(2):
+            d = 2 * g + half
+            for k in range(per):
+                u = c * per + k
+                part = pl.ds(u * UNIT, UNIT)
+
+                @pl.when(u == units - 1)
+                def _():
+                    put(half, k, tail.at[partner(d)[0]]).start()
+
+                @pl.when((u != units - 1) & (d == 0))
+                def _():
+                    put(half, k, back.at[me, part]).start()
+
+                @pl.when((u != units - 1) & (d != 0))
+                def _():
+                    put(half, k, staged.at[d, part]).start()
+
+        for half in range(2):
+            d = 2 * g + half
+            for k in range(per):
+                u = c * per + k
+                put(half, k, tail.at[me]).wait()
+
+                @pl.when((u != units - 1) & (d != 0))
+                def _():
+                    to_owner(d, u).start()
         return carry
 
     lax.fori_loop(0, CHUNKS * num_experts // 2, step, 0)
@@ -272,7 +363,7 @@
 
     def gate_step(i, carry):
         for half in range(2):
-            got = pltpu.make_async_copy(tokens.at[pl.ds((2 * i + half) * cg, cg)], x.at[half], sem_x.at[half])
+            got = pltpu.make_async_copy(tokens.at[pl.ds((2 * i + half) * cg, cg)], x.at[half], sem_x.at[half, 0])
             got.start()
             got.wait()
         proj = jnp.dot(x[...].reshape(prob.shape[0], x.shape[3]), wr_ref[...], preferred_element_type=jnp.float32)
@@ -281,33 +372,36 @@
         top = jnp.max(jnp.where(real, logits, -jnp.inf), axis=1, keepdims=True)
         weight = jnp.where(real, jnp.exp(logits - top), 0.0)
         prob[...] = weight / jnp.sum(weight, axis=1, keepdims=True)
-        put = pltpu.make_async_copy(prob, probs.at[pl.ds(i * prob.shape[0], prob.shape[0])], sem_y.at[0])
+        put = pltpu.make_async_copy(prob, probs.at[pl.ds(i * prob.shape[0], prob.shape[0])], sem_y.at[0, 0])
         put.start()
         put.wait()
         return carry
 
     lax.fori_loop(0, probs.shape[0] // prob.shape[0], gate_step, 0)
-    for c in range(CHUNKS):
+    for u in range(1, units):
         for d in range(1, num_experts):
-            to_expert(d, c).wait_send()
-            to_owner(d, c).wait()
-
-
-def exchange(send, w_first, b_first, w_second, b_second, tok_rows, w_route, expert_keys, tau):
+            to_expert(d, u).wait_send()
+    for u in range(units - 1):
+        for d in range(1, num_experts):
+            to_owner(d, u).wait()
+
+
+def exchange(first, send, w_first, b_first, w_second, b_second, tok_rows, w_route, expert_keys, tau):
     num_experts, slot_groups, _, width = send.shape
     tok = tok_rows.shape[0]
     hidden = w_first.shape[1]
     cg = slot_groups // CHUNKS
     land = jax.ShapeDtypeStruct((num_experts, slot_groups, GRP, width), jnp.bfloat16)
+    tail = jax.ShapeDtypeStruct((num_experts, UNIT, GRP, width), jnp.bfloat16)
     probs = jax.ShapeDtypeStruct((tok, 128), jnp.float32)
-    sems = pltpu.SemaphoreType.DMA((num_experts, CHUNKS))
+    sems = pltpu.SemaphoreType.DMA((num_experts, slot_groups // UNIT))
     hbm = pl.BlockSpec(memory_space=pl.ANY)
     vmem = pl.BlockSpec(memory_space=pltpu.VMEM)
     return pl.pallas_call(
         functools.partial(exchange_kernel, num_experts, slot_groups),
-        out_shape=(land, land, land, probs),
-        in_specs=[hbm, hbm, vmem, hbm, vmem, hbm, vmem, vmem, pl.BlockSpec(memory_space=pltpu.SMEM)],
-        out_specs=(hbm, hbm, hbm, hbm),
+        out_shape=(land, land, land, tail, probs),
+        in_specs=[hbm, hbm, hbm, vmem, hbm, vmem, hbm, vmem, vmem, pl.BlockSpec(memory_space=pltpu.SMEM)],
+        out_specs=(hbm, hbm, hbm, hbm, hbm),
         scratch_shapes=[
             pltpu.VMEM((width, hidden), jnp.bfloat16),
             pltpu.VMEM((hidden, width), jnp.bfloat16),
@@ -316,41 +410,35 @@
             pltpu.VMEM((2 * cg * GRP, hidden), jnp.bfloat16),
             pltpu.VMEM((2 * cg * GRP, 128), jnp.float32),
             pltpu.SemaphoreType.DMA((2,)),
-            pltpu.SemaphoreType.DMA((2,)),
-            pltpu.SemaphoreType.DMA((2,)),
+            pltpu.SemaphoreType.DMA((2, cg // UNIT)),
+            pltpu.SemaphoreType.DMA((2, cg // UNIT)),
             sems, sems, sems, sems,
         ],
         compiler_params=pltpu.CompilerParams(collective_id=0, has_side_effects=True, vmem_limit_bytes=60 * 2**20),
         name="exchange",
-    )(send, w_first, b_first[None], w_second, b_second[None], tok_rows.reshape(tok // GRP, GRP, width), w_route, expert_keys, tau.reshape(1, 1))
-
-
-def combine_kernel(num_experts, meta_ref, back_ref, code_ref, prob_ref, o_ref, rows_in, sem):
+    )(first, send, w_first, b_first[None], w_second, b_second[None], tok_rows.reshape(tok // GRP, GRP, width), w_route, expert_keys, tau.reshape(1, 1))
+
+
+def combine_kernel(num_experts, final, meta_ref, back_ref, tail_ref, code_ref, prob_ref, o_ref, rows_in, sem):
+    early = meta_ref[5, 0]
+    first = early if final else 0
     i, last = pl.program_id(0), pl.num_programs(0) - 1
     span = WIN // GRP
     width = o_ref.shape[1]
+    units = sem.shape[1]
     cols = lax.broadcasted_iota(jnp.int32, (BLK, 128), 1)
     row = lax.broadcasted_iota(jnp.int32, (WIN, width), 0)
 
-    def unit(e, u):
+    def unit(e, u, from_tail=False):
         part = pl.ds(u * UNIT, UNIT)
-        return pltpu.make_async_copy(back_ref.at[e, part], rows_in.at[e, part], sem.at[e, u])
-
-    @pl.when(i == 0)
-    def _():
-        for u in range(back_ref.shape[1] // UNIT):
-            for e in range(num_experts):
-                @pl.when(u < used_units(meta_ref, e))
-                def _():
-                    unit(e, u).start()
+        return pltpu.make_async_copy(tail_ref.at[e] if from_tail else back_ref.at[e, part], rows_in.at[e, part], sem.at[e, u])
+
+    def rows_before(step, e):
+        n = step * STEP * num_experts + e
+        return meta_ref[0, n] * GRP + meta_ref[3, n]
 
     def reach(step, e):
-        n = (meta_ref[0, step * STEP * num_experts + e] * GRP + meta_ref[3, step * STEP * num_experts + e] + (UNIT * GRP - 1)) // (UNIT * GRP)
-        return n
-
-    for e in range(num_experts):
-        end = jnp.where(i == last, used_units(meta_ref, e), reach(jnp.minimum(i + 1, last), e))
-        lax.fori_loop(reach(i, e), end, lambda u, c, e=e: (unit(e, u).wait(), c)[1], 0)
+        return (rows_before(step, e) + (UNIT * GRP - 1)) // (UNIT * GRP)
 
     def block(k, carry):
         b = i * STEP + k
@@ -377,32 +465,70 @@
 
         return lax.fori_loop(1, most(meta_ref, b, num_experts), more, carry)
 
-    lax.fori_loop(0, STEP, block, 0)
-
-
-def combine(back, code, meta, probs):
+    @pl.when(i == first)
+    def _():
+        for u in range(units if final else units - 1):
+            for e in range(num_experts):
+                if final:
+                    wanted = (u >= rows_before(early, e) // (UNIT * GRP)) & (u < used_units(meta_ref, e))
+                else:
+                    wanted = u < reach(early, e)
+
+                @pl.when(wanted)
+                def _():
+                    unit(e, u, u == units - 1).start()
+
+    @pl.when((i >= early) if final else (i < early))
+    def _():
+        for e in range(num_experts):
+            begin = reach(i, e)
+            end = reach(jnp.minimum(i + 1, last), e)
+            if final:
+                begin = jnp.where(i == early, rows_before(early, e) // (UNIT * GRP), begin)
+                end = jnp.where(i == last, used_units(meta_ref, e), end)
+            lax.fori_loop(begin, end, lambda u, c, e=e: (unit(e, u).wait(), c)[1], 0)
+        lax.fori_loop(0, STEP, block, 0)
+
+
+def combine(back, tail, code, meta, probs, out=None):
     tok, width = probs.shape[0], back.shape[3]
     num_experts, slot_groups = back.shape[:2]
+    final = out is not None
+    steps = tok // (BLK * STEP)
+    kernel = functools.partial(combine_kernel, num_experts, final)
+    hbm = pl.BlockSpec(memory_space=pl.ANY)
+
+    def mine(i, meta_ref):
+        return (jnp.maximum(i, meta_ref[5, 0]), 0) if final else (jnp.minimum(i, jnp.maximum(meta_ref[5, 0] - 1, 0)), 0)
+
+    def call(meta_ref, *refs):
+        if final:
+            back_ref, tail_ref, code_ref, prob_ref, _, *rest = refs
+        else:
+            back_ref, code_ref, prob_ref, *rest = refs
+            tail_ref = None
+        kernel(meta_ref, back_ref, tail_ref, code_ref, prob_ref, *rest)
+
+    table = pl.BlockSpec(code.shape, lambda i, *_: (0, 0))
+    gates = pl.BlockSpec((STEP * BLK, 128), mine)
     return pl.pallas_call(
-        functools.partial(combine_kernel, num_experts),
+        call,
         grid_spec=pltpu.PrefetchScalarGridSpec(
             num_scalar_prefetch=1,
-            grid=(tok // (BLK * STEP),),
-            in_specs=[
-                pl.BlockSpec(memory_space=pl.ANY),
-                pl.BlockSpec(code.shape, lambda i, *_: (0, 0)),
-                pl.BlockSpec((STEP * BLK, 128), lambda i, *_: (i, 0)),
-            ],
-            out_specs=pl.BlockSpec((STEP * BLK, width), lambda i, *_: (i, 0)),
+            grid=(steps,),
+            in_specs=[hbm, hbm, table, gates, hbm] if final else [hbm, table, gates],
+            out_specs=pl.BlockSpec((STEP * BLK, width), mine),
             scratch_shapes=[
                 pltpu.VMEM((num_experts, slot_groups + WIN // GRP, GRP, width), jnp.bfloat16),
                 pltpu.SemaphoreType.DMA((num_experts, slot_groups // UNIT)),
             ],
         ),
         out_shape=jax.ShapeDtypeStruct((tok, width), jnp.bfloat16),
+        input_output_aliases={5: 0} if final else {},
         compiler_params=pltpu.CompilerParams(vmem_limit_bytes=56 * 2**20),
-        name="combine",
-    )(meta, back, code, probs)
+        cost_estimate=pl.CostEstimate(flops=2 * tok * num_experts * WIN * width, bytes_accessed=5 * tok * width, transcendentals=0),
+        name="combine_final" if final else "combine",
+    )(*((meta, back, tail, code, probs, out) if final else (meta, back, code, probs)))
 
 
 def solution(mesh):
@@ -414,11 +540,15 @@
         tok_rows, id_row = tokens[0], expert_ids[0]
         tok, width = tok_rows.shape
         capacity = (5 * tok + 4 * num_experts - 1) // (4 * num_experts)
-        slot_groups = -(-capacity // (GRP * CHUNKS)) * CHUNKS
+        slot_groups = -(-capacity // (GRP * UNIT * CHUNKS)) * UNIT * CHUNKS
         code, meta = route(route_order[0], id_row, num_experts, capacity)
-        send = dispatch(tok_rows, code, meta, num_experts, slot_groups)
-        back, _, _, probs = exchange(send, w_in[0], b_in[0], w_out[0], b_out[0], tok_rows, w_route, expert_keys, tau)
-        return combine(back, code, meta, probs)[None]
+        first = dispatch_first(tok_rows, code, meta, num_experts)
+        send = dispatch(tok_rows, code, meta, first, slot_groups)
+        first = lax.all_to_all(first, EXPERT_AXES, 0, 0, tiled=True)
+        back, _, _, tail, probs = exchange(first, send, w_in[0], b_in[0], w_out[0], b_out[0], tok_rows, w_route, expert_keys, tau)
+        tail = lax.all_to_all(tail, EXPERT_AXES, 0, 0, tiled=True)
+        out = combine(back, None, code, meta, probs)
+        return combine(back, tail, code, meta, probs, out)[None]
 
     return jax.shard_map(
         device_step,

time: 638 us -> 614 us (0.962)
  Pallas kernels: 632 us -> 587 us
  waiting for transfers between devices: 0 us -> 12.5 us
  starting transfers between devices: 0 us -> 6.68 us
    pallas_call x1, Pallas kernels: 572 us -> 514 us  [exchange(): pl.pallas_call(functools.partial(exchange_kernel, num_experts, slot_group...]
    pallas_call x1 -> x3, Pallas kernels: 28.8 us -> 42.5 us  [the longest x2 35.2 us: combine(): pl.pallas_call(call, grid_spec=pltpu.PrefetchScalarGridSpec(num_scalar_pr...]
    all_to_all x0 -> x2, waiting for transfers between devices: none -> 12.5 us  [the longest x1 6.52 us: device_step(): tail = lax.all_to_all(tail, EXPERT_AXES, 0, 0, tiled=True)]
    all_to_all x0 -> x2, starting transfers between devices: none -> 6.68 us  [the longest x1 4.31 us: device_step(): first = lax.all_to_all(first, EXPERT_AXES, 0, 0, tiled=True)]
  transfers between devices with their start and end apart: 0 -> 2, of which waited for: 0 -> 2; matrix products, arithmetic and copies ran while one was open for 0% -> 0% of each run, Pallas kernels for 0% -> 8%
where the time goes in v3:
time: 614 us; the launch traced here: 612 us
  Pallas kernels  587 us (96%)
  waiting for transfers between devices  12.5 us (2%)
  starting transfers between devices  6.68 us (1%)
    pallas_call x1, Pallas kernels, exchange(): pl.pallas_call(functools.partial(exchange_kernel, num_experts, slot_group...  514 us
    pallas_call x2, Pallas kernels, combine(): pl.pallas_call(call, grid_spec=pltpu.PrefetchScalarGridSpec(num_scalar_pr...  35.2 us
    pallas_call x1, Pallas kernels, dispatch(): pl.pallas_call(functools.partial(dispatch_kernel, num_experts), grid_spec...  25.6 us
  transfers between devices with their start and end apart: 2, of which 2 were waited for; matrix products, arithmetic and copies ran while one was open for 0% of the time, Pallas kernels for 8%

profile of v3, /device:TPU:0, one launch (start us, length us, event | category | flops | bytes accessed | tf_op | source)
XLA Modules:
  0.0 611.7 jit_solution(6194691017739931294)
XLA Ops:
  0.0 5.4 route.1
  5.4 0.0 copy-start
  5.4 0.8 copy-done
  6.1 0.0 copy-start.2
  6.1 0.7 copy-done.2
  6.8 0.0 copy-start.1
  6.8 0.0 copy-start.3
  6.8 7.2 %dispatch_first.1._ = bf16[8,8,16,1280]{3,2,1,0:T(8,128)(2,1)} custom-call(s32[8,256]{1,0:T(8,128)S(1)} %copy-done.2, bf16[8192,1280]{1,0:T(8,128)(2,1)} %bitcast.8, s32[32,256]{1,0:T(8,128)S(1)} %copy-done), custom_call_target="tpu_custom_call" | custom-call | tf_op jit(solution)/shard_map/dispatch_first/pallas_call | solution.py:176
  14.1 4.3 all-to-all-start
  19.1 0.0 copy-done.1
  19.1 0.0 copy-done.3
  19.1 25.6 %dispatch.1.send = bf16[8,80,16,1280]{3,2,1,0:T(8,128)(2,1)} custom-call(s32[8,256]{1,0:T(8,128)S(1)} %copy-done.3, bf16[8192,1280]{1,0:T(8,128)(2,1)} %bitcast.9, s32[32,256]{1,0:T(8,128)S(1)} %copy-done.1, bf16[8,8,16,1280]{3,2,1,0:T(8,128)(2,1)} %dispatch_first.1._), custom_call_target="tpu_custom_call" | custom-call | flops 10737418240 | bytes 52428800 | tf_op jit(solution)/shard_map/dispatch/pallas_call | solution.py:223
  44.6 6.0 all-to-all-done.first
  50.6 0.0 copy-start.4
  50.6 1.5 copy-done.4
  52.1 513.8 %exchange.1 = (bf16[8,80,16,1280]{3,2,1,0:T(8,128)(2,1)}, bf16[8,80,16,1280]{3,2,1,0:T(8,128)(2,1)}, bf16[8,80,16,1280]{3,2,1,0:T(8,128)(2,1)}, bf16[8,8,16,1280]{3,2,1,0:T(8,128)(2,1)}, f32[8192,128]{1,0:T(8,128)}) custom-call(bf16[8,8,16,1280]{3,2,1,0:T(8,128)(2,1)} %copy-done.4, bf16[8,80,16,1280]{3,2,1,0:T(8,128)(2,1)} %dispatch.1.send, ...), custom_call_target="tpu_custom_call" | custom-call | tf_op jit(solution)/shard_map/exchange/pallas_call | solution.py:400
  565.9 2.4 all-to-all-start.1
  568.3 25.6 %combine.1.refs_4_ = bf16[8192,1280]{1,0:T(8,128)(2,1)} custom-call(s32[8,256]{1,0:T(8,128)} %get-tuple-element.10.meta_ref, bf16[8,80,16,1280]{3,2,1,0:T(8,128)(2,1)} %get-tuple-element.12.refs_0_, s32[32,256]{1,0:T(8,128)} %get-tuple-element.11.code_ref.refs_1_.refs_2_, f32[8192,128]{1,0:T(8,128)} %get-tuple-element.14.refs_2_.refs_3_), custom_call_target="tpu_custom_call" | custom-call | flops 10737418240 | bytes 52428800 | tf_op jit(solution)/shard_map/combine/pallas_call | solution.py:514
  594.0 6.5 %all-to-all-done.1.refs_1_ = bf16[8,8,16,1280]{3,2,1,0:T(8,128)(2,1)S(1)} async-done(((bf16[8,8,16,1280]{3,2,1,0:T(8,128)(2,1)}), bf16[8,8,16,1280]{3,2,1,0:T(8,128)(2,1)S(1)}, u32[]{:S(2)}, u32[]{:S(2)}) %all-to-all-start.1) | async-done | bytes 2621472 | tf_op jit(solution)/shard_map/all_to_all | solution.py:549
  600.5 0.0 copy-start.5
  600.5 1.5 copy-done.5
  602.0 9.6 %combine_final.1 = bf16[8192,1280]{1,0:T(8,128)(2,1)} custom-call(s32[8,256]{1,0:T(8,128)} %get-tuple-element.10.meta_ref, bf16[8,80,16,1280]{3,2,1,0:T(8,128)(2,1)} %get-tuple-element.12.refs_0_, bf16[8,8,16,1280]{3,2,1,0:T(8,128)(2,1)} %copy-done.5, s32[32,256]{1,0:T(8,128)} %get-tuple-element.11.code_ref.refs_1_.refs_2_, ...), custom_call_target="tpu_custom_call", output_to_operand_aliasing={{}: (5, {})} | custom-call | flops 10737418240 | bytes 52428800 | tf_op jit(solution)/shard_map/combine_final/pallas_call | solution.py:514
Async XLA Ops:
  5.4 0.8 copy-start
  6.1 0.7 copy-start.2
  6.8 12.2 %copy-start.1 = (s32[32,256]{1,0:T(8,128)S(1)}, s32[32,256]{1,0:T(8,128)}, u32[]{:S(2)}) copy-start(s32[32,256]{1,0:T(8,128)} %get-tuple-element.11.code_ref.refs_1_.refs_2_) | copy-start | bytes 98308
  6.8 12.2 %copy-start.3 = (s32[8,256]{1,0:T(8,128)S(1)}, s32[8,256]{1,0:T(8,128)}, u32[]{:S(2)}) copy-start(s32[8,256]{1,0:T(8,128)} %get-tuple-element.10.meta_ref) | copy-start | bytes 24580
  14.1 36.5 %all-to-all-start = ((bf16[8,8,16,1280]{3,2,1,0:T(8,128)(2,1)}), bf16[8,8,16,1280]{3,2,1,0:T(8,128)(2,1)S(1)}, u32[]{:S(2)}, u32[]{:S(2)}) async-start(bf16[8,8,16,1280]{3,2,1,0:T(8,128)(2,1)} %dispatch_first.1._), calls=%async_computation | async-start | bytes 5242880 | tf_op jit(solution)/shard_map/all_to_all | solution.py:547
  50.6 1.5 copy-start.4
  565.9 34.5 %all-to-all-start.1 = ((bf16[8,8,16,1280]{3,2,1,0:T(8,128)(2,1)}), bf16[8,8,16,1280]{3,2,1,0:T(8,128)(2,1)S(1)}, u32[]{:S(2)}, u32[]{:S(2)}) async-start(bf16[8,8,16,1280]{3,2,1,0:T(8,128)(2,1)} %get-tuple-element.13), calls=%async_computation.1 | async-start | bytes 5242880 | tf_op jit(solution)/shard_map/all_to_all | solution.py:549
  600.5 1.5 copy-start.5

commit v4 on v3

--- a/solution.py
+++ b/solution.py
@@ -22,7 +22,41 @@
     return jnp.where(mask, 1.0, 0.0)
 
 
-def route_kernel(num_experts, capacity, order_ref, ids_ref, grid_ref, code_ref, meta_ref, hot, keep):
+def most(meta_ref, b, num_experts):
+    n = meta_ref[1, b * num_experts]
+    for e in range(1, num_experts):
+        n = jnp.maximum(n, meta_ref[1, b * num_experts + e])
+    return n
+
+
+def place(num_experts, meta_ref, b, code, x, acc):
+    span = WIN // GRP
+    width = x.shape[1]
+    rows = lax.broadcasted_iota(jnp.int32, (num_experts * WIN, BLK), 0)
+    sub = lax.broadcasted_iota(jnp.int32, (GRP, width), 0)
+
+    def one_pass(p, carry):
+        sel = onehot(rows == code - p * (num_experts * WIN)).astype(jnp.bfloat16)
+        win = jnp.dot(sel, x, preferred_element_type=jnp.float32).astype(jnp.bfloat16)
+        win = win.reshape(num_experts, span, GRP, width)
+        for e in range(num_experts):
+            at = jnp.minimum(meta_ref[0, b * num_experts + e] + p * span, acc.shape[1] - span)
+            old = jnp.where(p == 0, meta_ref[3, b * num_experts + e], 0)
+            acc[e, at] = jnp.where(sub < old, acc[e, at], win[e, 0])
+            acc[e, pl.ds(at + 1, span - 1)] = win[e, 1:]
+        return carry
+
+    lax.fori_loop(0, most(meta_ref, b, num_experts), one_pass, 0)
+
+
+def route_kernel(num_experts, capacity, order_ref, ids_ref, grid_ref, x_ref, code_ref, meta_ref, o_ref, hot, keep, meta, slots, ring, sem_x, sem_o):
+    depth = ring.shape[0]
+
+    def load(b):
+        return pltpu.make_async_copy(x_ref.at[pl.ds(pl.multiple_of(b * BLK, BLK), BLK)], ring.at[b % depth], sem_x.at[b % depth])
+
+    for b in range(depth):
+        load(b).start()
     tok = order_ref.shape[1]
     blocks = tok // BLK
     rows = blocks * num_experts
@@ -86,107 +120,74 @@
     ahead = onehot(start[:, :1] <= (capacity - UNIT * GRP) // (UNIT * GRP) * (UNIT * GRP))
     for b in range(STEP, blocks, STEP):
         early += jnp.min(ahead[b * num_experts:(b + 1) * num_experts], axis=0, keepdims=True)
-    needed = jnp.ones((1, 1), jnp.float32)
+    fill = jnp.ones((1, 1), jnp.float32)
     behind = onehot(start[:, :1] < UNIT * GRP)
     for b in range(1, blocks):
-        needed += jnp.max(behind[b * num_experts:(b + 1) * num_experts], axis=0, keepdims=True)
-    meta_ref[6:7, :] = jnp.broadcast_to(needed, (1, rows)).astype(jnp.int32)
+        fill += jnp.max(behind[b * num_experts:(b + 1) * num_experts], axis=0, keepdims=True)
+    meta_ref[7:8, :] = jnp.zeros((1, rows), jnp.int32)
+    meta_ref[6:7, :] = jnp.broadcast_to(fill, (1, rows)).astype(jnp.int32)
     meta_ref[5:6, :] = jnp.broadcast_to(early, (1, rows)).astype(jnp.int32)
     for row, value in enumerate((base, need, total, local, local + count.astype(jnp.int32))):
         wide = jnp.broadcast_to(value[:, :1], (rows, 128)).astype(jnp.float32)
         meta_ref[row:row + 1, :] = jnp.transpose(wide)[:1].astype(jnp.int32)
-
-
-def route(order_row, id_row, num_experts, capacity):
-    tok = order_row.shape[0]
-    blocks = tok // BLK
-    rows = blocks * num_experts
-    return pl.pallas_call(
-        functools.partial(route_kernel, num_experts, capacity),
-        out_shape=(jax.ShapeDtypeStruct((blocks, BLK), jnp.int32), jax.ShapeDtypeStruct((8, rows), jnp.int32)),
-        scratch_shapes=[pltpu.VMEM((rows, BLK), jnp.float32), pltpu.VMEM((tok // 128, 128), jnp.float32)],
-        name="route",
-    )(order_row[None], id_row[None], id_row.reshape(tok // 128, 128))
-
-
-def most(meta_ref, b, num_experts):
-    n = meta_ref[1, b * num_experts]
-    for e in range(1, num_experts):
-        n = jnp.maximum(n, meta_ref[1, b * num_experts + e])
-    return n
-
-
-def used_units(meta_ref, e):
-    return (meta_ref[2, e] + (UNIT * GRP - 1)) // (UNIT * GRP)
-
-
-def place(num_experts, meta_ref, b, code, x, acc):
-    span = WIN // GRP
-    width = x.shape[1]
-    rows = lax.broadcasted_iota(jnp.int32, (num_experts * WIN, BLK), 0)
-    sub = lax.broadcasted_iota(jnp.int32, (GRP, width), 0)
-
-    def one_pass(p, carry):
-        sel = onehot(rows == code - p * (num_experts * WIN)).astype(jnp.bfloat16)
-        win = jnp.dot(sel, x, preferred_element_type=jnp.float32).astype(jnp.bfloat16)
-        win = win.reshape(num_experts, span, GRP, width)
-        for e in range(num_experts):
-            at = jnp.minimum(meta_ref[0, b * num_experts + e] + p * span, acc.shape[1] - span)
-            old = jnp.where(p == 0, meta_ref[3, b * num_experts + e], 0)
-            acc[e, at] = jnp.where(sub < old, acc[e, at], win[e, 0])
-            acc[e, pl.ds(at + 1, span - 1)] = win[e, 1:]
-        return carry
-
-    lax.fori_loop(0, most(meta_ref, b, num_experts), one_pass, 0)
-
-
-def first_kernel(num_experts, meta_ref, x_ref, code_ref, o_ref, acc, ring, sem_x, sem_o):
-    blocks = meta_ref[6, 0]
-    depth = ring.shape[0]
-
-    def load(b):
-        return pltpu.make_async_copy(x_ref.at[pl.ds(pl.multiple_of(b * BLK, BLK), BLK)], ring.at[b % depth], sem_x.at[b % depth])
-
-    for b in range(depth):
-        @pl.when(b < blocks)
-        def _():
-            load(b).start()
+    share = pltpu.make_async_copy(meta_ref, meta, sem_o.at[0])
+    share.start()
+    share.wait()
+    needed = meta[6, 0]
 
     def block(b, carry):
         load(b).wait()
-        place(num_experts, meta_ref, b, code_ref[pl.ds(b, 1), :], ring[b % depth], acc)
-
-        @pl.when(b + depth < blocks)
+        place(num_experts, meta, b, code_ref[pl.ds(b, 1), :], ring[b % depth], slots)
+
+        @pl.when(b + depth < needed)
         def _():
             load(b + depth).start()
 
         return carry
 
-    lax.fori_loop(0, blocks, block, 0)
-    outs = [pltpu.make_async_copy(acc.at[e, pl.ds(0, UNIT)], o_ref.at[e], sem_o.at[e]) for e in range(num_experts)]
+    lax.fori_loop(0, needed, block, 0)
+    for b in range(depth):
+        @pl.when(b >= needed)
+        def _():
+            load(b).wait()
+    outs = [pltpu.make_async_copy(slots.at[e, pl.ds(0, UNIT)], o_ref.at[e], sem_o.at[e]) for e in range(num_experts)]
     for out in outs:
         out.start()
     for out in outs:
         out.wait()
 
 
-def dispatch_first(tok_rows, code, meta, num_experts):
-    width = tok_rows.shape[1]
-    depth = 8
+def route(order_row, id_row, tok_rows, num_experts, capacity):
+    tok, width = tok_rows.shape
+    blocks = tok // BLK
+    rows = blocks * num_experts
+    depth = min(8, blocks)
+    hbm = pl.BlockSpec(memory_space=pl.ANY)
     return pl.pallas_call(
-        functools.partial(first_kernel, num_experts),
-        in_specs=[pl.BlockSpec(memory_space=pltpu.SMEM), pl.BlockSpec(memory_space=pl.ANY), pl.BlockSpec(memory_space=pltpu.VMEM)],
-        out_specs=pl.BlockSpec(memory_space=pl.ANY),
-        out_shape=jax.ShapeDtypeStruct((num_experts, UNIT, GRP, width), jnp.bfloat16),
+        functools.partial(route_kernel, num_experts, capacity),
+        in_specs=[pl.BlockSpec(), pl.BlockSpec(), pl.BlockSpec(), hbm],
+        out_specs=(pl.BlockSpec(), pl.BlockSpec(), hbm),
+        out_shape=(
+            jax.ShapeDtypeStruct((blocks, BLK), jnp.int32),
+            jax.ShapeDtypeStruct((8, rows), jnp.int32),
+            jax.ShapeDtypeStruct((num_experts, UNIT, GRP, width), jnp.bfloat16),
+        ),
         scratch_shapes=[
+            pltpu.VMEM((rows, BLK), jnp.float32),
+            pltpu.VMEM((tok // 128, 128), jnp.float32),
+            pltpu.SMEM((8, rows), jnp.int32),
             pltpu.VMEM((num_experts, UNIT + WIN // GRP, GRP, width), jnp.bfloat16),
             pltpu.VMEM((depth, BLK, width), jnp.bfloat16),
             pltpu.SemaphoreType.DMA((depth,)),
             pltpu.SemaphoreType.DMA((num_experts,)),
         ],
-        compiler_params=pltpu.CompilerParams(vmem_limit_bytes=32 * 2**20),
-        name="dispatch_first",
-    )(meta, tok_rows, code)
+        compiler_params=pltpu.CompilerParams(vmem_limit_bytes=63 * 2**20),
+        name="route",
+    )(order_row[None], id_row[None], id_row.reshape(tok // 128, 128), tok_rows)
+
+
+def used_units(meta_ref, e):
+    return (meta_ref[2, e] + (UNIT * GRP - 1)) // (UNIT * GRP)
 
 
 def dispatch_kernel(num_experts, meta_ref, x_ref, code_ref, _, o_ref, acc, sem):
@@ -237,7 +238,7 @@
             ],
         ),
         out_shape=jax.ShapeDtypeStruct((num_experts, slot_groups, GRP, width), jnp.bfloat16),
-        compiler_params=pltpu.CompilerParams(vmem_limit_bytes=48 * 2**20),
+        compiler_params=pltpu.CompilerParams(vmem_limit_bytes=63 * 2**20),
         cost_estimate=pl.CostEstimate(flops=2 * tok * num_experts * WIN * width, bytes_accessed=5 * tok * width, transcendentals=0),
         name="dispatch",
     )(meta, tok_rows, code, first)
@@ -270,7 +271,7 @@
         pl.semaphore_signal(barrier, inc=1, device_id=partner(d)[1], device_id_type=MESH)
     pl.semaphore_wait(barrier, num_experts - 1)
 
-    far_first = (6, 7, 2, 3, 4, 5, 1)
+    far_first = (6, 4, 2, 7, 5, 3, 1)
     for u in range(1, units):
         for d in far_first:
             to_expert(d, u).start()
@@ -525,7 +526,7 @@
         ),
         out_shape=jax.ShapeDtypeStruct((tok, width), jnp.bfloat16),
         input_output_aliases={5: 0} if final else {},
-        compiler_params=pltpu.CompilerParams(vmem_limit_bytes=56 * 2**20),
+        compiler_params=pltpu.CompilerParams(vmem_limit_bytes=63 * 2**20),
         cost_estimate=pl.CostEstimate(flops=2 * tok * num_experts * WIN * width, bytes_accessed=5 * tok * width, transcendentals=0),
         name="combine_final" if final else "combine",
     )(*((meta, back, tail, code, probs, out) if final else (meta, back, code, probs)))
@@ -541,8 +542,7 @@
         tok, width = tok_rows.shape
         capacity = (5 * tok + 4 * num_experts - 1) // (4 * num_experts)
         slot_groups = -(-capacity // (GRP * UNIT * CHUNKS)) * UNIT * CHUNKS
-        code, meta = route(route_order[0], id_row, num_experts, capacity)
-        first = dispatch_first(tok_rows, code, meta, num_experts)
+        code, meta, first = route(route_order[0], id_row, tok_rows, num_experts, capacity)
         send = dispatch(tok_rows, code, meta, first, slot_groups)
         first = lax.all_to_all(first, EXPERT_AXES, 0, 0, tiled=True)
         back, _, _, tail, probs = exchange(first, send, w_in[0], b_in[0], w_out[0], b_out[0], tok_rows, w_route, expert_keys, tau)

time: 614 us -> 609 us (level)
    pallas_call x2 -> x1, Pallas kernels: 12.6 us -> 11 us  [route(): pl.pallas_call(functools.partial(route_kernel, num_experts, capacity), in...]
where the time goes in v4:
time: 609 us; the launch traced here: 607 us
  Pallas kernels  586 us (96%)
  waiting for transfers between devices  12.5 us (2%)
  starting transfers between devices  8.02 us (1%)
    pallas_call x1, Pallas kernels, exchange(): pl.pallas_call(functools.partial(exchange_kernel, num_experts, slot_group...  514 us
    pallas_call x2, Pallas kernels, combine(): pl.pallas_call(call, grid_spec=pltpu.PrefetchScalarGridSpec(num_scalar_pr...  35.4 us
    pallas_call x1, Pallas kernels, dispatch(): pl.pallas_call(functools.partial(dispatch_kernel, num_experts), grid_spec...  25.5 us
  transfers between devices with their start and end apart: 2, of which 2 were waited for; matrix products, arithmetic and copies ran while one was open for 0% of the time, Pallas kernels for 8%

profile of v4, /device:TPU:0, one launch (start us, length us, event | category | flops | bytes accessed | tf_op | source)
XLA Modules:
  0.0 607.1 jit_solution(9446432813671304508)
XLA Ops:
  0.0 11.0 %route.1 = (s32[32,256]{1,0:T(8,128)}, s32[8,256]{1,0:T(8,128)}, bf16[8,8,16,1280]{3,2,1,0:T(8,128)(2,1)}) custom-call(s32[1,8192]{1,0:T(1,128)} %order_ref.1, s32[1,8192]{1,0:T(1,128)} %ids_ref.1, s32[64,128]{1,0:T(8,128)} %bitcast.13, bf16[8192,1280]{1,0:T(8,128)(2,1)} %bitcast.8), custom_call_target="tpu_custom_call" | custom-call | tf_op jit(solution)/shard_map/route/pallas_call | solution.py:166
  11.0 4.9 all-to-all-start
  16.6 25.5 %dispatch.1.send = bf16[8,80,16,1280]{3,2,1,0:T(8,128)(2,1)} custom-call(s32[8,256]{1,0:T(8,128)} %get-tuple-element.11.meta_ref, bf16[8192,1280]{1,0:T(8,128)(2,1)} %bitcast.9, s32[32,256]{1,0:T(8,128)} %get-tuple-element.13.code_ref.refs_1_.refs_2_, bf16[8,8,16,1280]{3,2,1,0:T(8,128)(2,1)} %get-tuple-element.12._), custom_call_target="tpu_custom_call" | custom-call | flops 10737418240 | bytes 52428800 | tf_op jit(solution)/shard_map/dispatch/pallas_call | solution.py:224
  42.1 6.4 %all-to-all-done.first = bf16[8,8,16,1280]{3,2,1,0:T(8,128)(2,1)} async-done(((bf16[8,8,16,1280]{3,2,1,0:T(8,128)(2,1)}), bf16[8,8,16,1280]{3,2,1,0:T(8,128)(2,1)}, u32[]{:S(2)}, u32[]{:S(2)}) %all-to-all-start) | async-done | bytes 2621472 | tf_op jit(solution)/shard_map/all_to_all | solution.py:547
  48.5 513.7 %exchange.1 = (bf16[8,80,16,1280]{3,2,1,0:T(8,128)(2,1)}, bf16[8,80,16,1280]{3,2,1,0:T(8,128)(2,1)}, bf16[8,80,16,1280]{3,2,1,0:T(8,128)(2,1)}, bf16[8,8,16,1280]{3,2,1,0:T(8,128)(2,1)}, f32[8192,128]{1,0:T(8,128)}) custom-call(bf16[8,8,16,1280]{3,2,1,0:T(8,128)(2,1)} %all-to-all-done.first, bf16[8,80,16,1280]{3,2,1,0:T(8,128)(2,1)} %dispatch.1.send, ...), custom_call_target="tpu_custom_call" | custom-call | tf_op jit(solution)/shard_map/exchange/pallas_call | solution.py:401
  562.2 3.1 all-to-all-start.1
  565.3 26.0 %combine.1.refs_4_ = bf16[8192,1280]{1,0:T(8,128)(2,1)} custom-call(s32[8,256]{1,0:T(8,128)} %get-tuple-element.11.meta_ref, bf16[8,80,16,1280]{3,2,1,0:T(8,128)(2,1)} %get-tuple-element.14.refs_0_, s32[32,256]{1,0:T(8,128)} %get-tuple-element.13.code_ref.refs_1_.refs_2_, f32[8192,128]{1,0:T(8,128)} %get-tuple-element.16.refs_2_.refs_3_), custom_call_target="tpu_custom_call" | custom-call | flops 10737418240 | bytes 52428800 | tf_op jit(solution)/shard_map/combine/pallas_call | solution.py:515
  591.4 6.1 %all-to-all-done.1.refs_1_ = bf16[8,8,16,1280]{3,2,1,0:T(8,128)(2,1)} async-done(((bf16[8,8,16,1280]{3,2,1,0:T(8,128)(2,1)}), bf16[8,8,16,1280]{3,2,1,0:T(8,128)(2,1)}, u32[]{:S(2)}, u32[]{:S(2)}) %all-to-all-start.1) | async-done | bytes 2621472 | tf_op jit(solution)/shard_map/all_to_all | solution.py:549
  597.5 9.4 %combine_final.1 = bf16[8192,1280]{1,0:T(8,128)(2,1)} custom-call(s32[8,256]{1,0:T(8,128)} %get-tuple-element.11.meta_ref, bf16[8,80,16,1280]{3,2,1,0:T(8,128)(2,1)} %get-tuple-element.14.refs_0_, bf16[8,8,16,1280]{3,2,1,0:T(8,128)(2,1)} %all-to-all-done.1.refs_1_, ...), custom_call_target="tpu_custom_call", output_to_operand_aliasing={{}: (5, {})} | custom-call | flops 10737418240 | bytes 52428800 | tf_op jit(solution)/shard_map/combine_final/pallas_call | solution.py:515
Async XLA Ops:
  11.0 37.5 %all-to-all-start = ((bf16[8,8,16,1280]{3,2,1,0:T(8,128)(2,1)}), bf16[8,8,16,1280]{3,2,1,0:T(8,128)(2,1)}, u32[]{:S(2)}, u32[]{:S(2)}) async-start(bf16[8,8,16,1280]{3,2,1,0:T(8,128)(2,1)} %get-tuple-element.12._), calls=%async_computation | async-start | bytes 5242880 | tf_op jit(solution)/shard_map/all_to_all | solution.py:547
  562.2 35.3 %all-to-all-start.1 = ((bf16[8,8,16,1280]{3,2,1,0:T(8,128)(2,1)}), bf16[8,8,16,1280]{3,2,1,0:T(8,128)(2,1)}, u32[]{:S(2)}, u32[]{:S(2)}) async-start(bf16[8,8,16,1280]{3,2,1,0:T(8,128)(2,1)} %get-tuple-element.15), calls=%async_computation.1 | async-start | bytes 5242880 | tf_op jit(solution)/shard_map/all_to_all | solution.py:549

commit v5 on v4

--- a/solution.py
+++ b/solution.py
@@ -10,7 +10,7 @@
 EXPERT_AXES = ("ep_b", "ep_a")
 CHUNKS = 5
 BLK = 256
-STEP = 4
+STEP = 2
 GRP = 16
 UNIT = 8
 WIN = 64

time: 609 us -> 610 us (level)
  waiting for transfers between devices: 12.5 us -> 5.83 us
  transfers between devices with their start and end apart: 2 -> 2, of which waited for: 2 -> 2; matrix products, arithmetic and copies ran while one was open for 0% -> 0% of each run, Pallas kernels for 8% -> 10%
where the time goes in v5:
time: 610 us; the launch traced here: 607 us
  Pallas kernels  592 us (97%)
  starting transfers between devices  8.01 us (1%)
    pallas_call x1, Pallas kernels, exchange(): pl.pallas_call(functools.partial(exchange_kernel, num_experts, slot_group...  514 us
    pallas_call x2, Pallas kernels, combine(): pl.pallas_call(call, grid_spec=pltpu.PrefetchScalarGridSpec(num_scalar_pr...  39.1 us
    pallas_call x1, Pallas kernels, dispatch(): pl.pallas_call(functools.partial(dispatch_kernel, num_experts), grid_spec...  28.3 us
  transfers between devices with their start and end apart: 2, of which 2 were waited for; matrix products, arithmetic and copies ran while one was open for 0% of the time, Pallas kernels for 10%

profile of v5, /device:TPU:0, one launch (start us, length us, event | category | flops | bytes accessed | tf_op | source)
XLA Modules:
  0.0 606.9 jit_solution(2477371833242463350)
XLA Ops:
  0.0 11.0 %route.1 = (s32[32,256]{1,0:T(8,128)}, s32[8,256]{1,0:T(8,128)}, bf16[8,8,16,1280]{3,2,1,0:T(8,128)(2,1)}) custom-call(s32[1,8192]{1,0:T(1,128)} %order_ref.1, s32[1,8192]{1,0:T(1,128)} %ids_ref.1, s32[64,128]{1,0:T(8,128)} %bitcast.13, bf16[8192,1280]{1,0:T(8,128)(2,1)} %bitcast.8), custom_call_target="tpu_custom_call" | custom-call | tf_op jit(solution)/shard_map/route/pallas_call | solution.py:166
  11.1 4.9 all-to-all-start
  16.6 28.3 %dispatch.1.send = bf16[8,80,16,1280]{3,2,1,0:T(8,128)(2,1)} custom-call(s32[8,256]{1,0:T(8,128)} %get-tuple-element.11.meta_ref, bf16[8192,1280]{1,0:T(8,128)(2,1)} %bitcast.9, s32[32,256]{1,0:T(8,128)} %get-tuple-element.13.code_ref.refs_1_.refs_2_, bf16[8,8,16,1280]{3,2,1,0:T(8,128)(2,1)} %get-tuple-element.12._), custom_call_target="tpu_custom_call" | custom-call | flops 10737418240 | bytes 52428800 | tf_op jit(solution)/shard_map/dispatch/pallas_call | solution.py:224
  44.9 3.2 all-to-all-done.first
  48.1 513.7 %exchange.1 = (bf16[8,80,16,1280]{3,2,1,0:T(8,128)(2,1)}, bf16[8,80,16,1280]{3,2,1,0:T(8,128)(2,1)}, bf16[8,80,16,1280]{3,2,1,0:T(8,128)(2,1)}, bf16[8,8,16,1280]{3,2,1,0:T(8,128)(2,1)}, f32[8192,128]{1,0:T(8,128)}) custom-call(bf16[8,8,16,1280]{3,2,1,0:T(8,128)(2,1)} %all-to-all-done.first, bf16[8,80,16,1280]{3,2,1,0:T(8,128)(2,1)} %dispatch.1.send, ...), custom_call_target="tpu_custom_call" | custom-call | tf_op jit(solution)/shard_map/exchange/pallas_call | solution.py:401
  561.8 3.1 all-to-all-start.1
  565.0 29.5 %combine.1.refs_4_ = bf16[8192,1280]{1,0:T(8,128)(2,1)} custom-call(s32[8,256]{1,0:T(8,128)} %get-tuple-element.11.meta_ref, bf16[8,80,16,1280]{3,2,1,0:T(8,128)(2,1)} %get-tuple-element.14.refs_0_, s32[32,256]{1,0:T(8,128)} %get-tuple-element.13.code_ref.refs_1_.refs_2_, f32[8192,128]{1,0:T(8,128)} %get-tuple-element.16.refs_2_.refs_3_), custom_call_target="tpu_custom_call" | custom-call | flops 10737418240 | bytes 52428800 | tf_op jit(solution)/shard_map/combine/pallas_call | solution.py:515
  594.5 2.6 all-to-all-done.1.refs_1_
  597.1 9.6 %combine_final.1 = bf16[8192,1280]{1,0:T(8,128)(2,1)} custom-call(s32[8,256]{1,0:T(8,128)} %get-tuple-element.11.meta_ref, bf16[8,80,16,1280]{3,2,1,0:T(8,128)(2,1)} %get-tuple-element.14.refs_0_, bf16[8,8,16,1280]{3,2,1,0:T(8,128)(2,1)} %all-to-all-done.1.refs_1_, ...), custom_call_target="tpu_custom_call", output_to_operand_aliasing={{}: (5, {})} | custom-call | flops 10737418240 | bytes 52428800 | tf_op jit(solution)/shard_map/combine_final/pallas_call | solution.py:515
Async XLA Ops:
  11.1 37.1 %all-to-all-start = ((bf16[8,8,16,1280]{3,2,1,0:T(8,128)(2,1)}), bf16[8,8,16,1280]{3,2,1,0:T(8,128)(2,1)}, u32[]{:S(2)}, u32[]{:S(2)}) async-start(bf16[8,8,16,1280]{3,2,1,0:T(8,128)(2,1)} %get-tuple-element.12._), calls=%async_computation | async-start | bytes 5242880 | tf_op jit(solution)/shard_map/all_to_all | solution.py:547
  561.8 35.3 %all-to-all-start.1 = ((bf16[8,8,16,1280]{3,2,1,0:T(8,128)(2,1)}), bf16[8,8,16,1280]{3,2,1,0:T(8,128)(2,1)}, u32[]{:S(2)}, u32[]{:S(2)}) async-start(bf16[8,8,16,1280]{3,2,1,0:T(8,128)(2,1)} %get-tuple-element.15), calls=%async_computation.1 | async-start | bytes 5242880 | tf_op jit(solution)/shard_map/all_to_all | solution.py:549
